TPU v7x, 32 devices: a whole 2x2x4 slice. The times are simulated.
32 devices in a mesh: dp: 8 (over z, x), tensor: 4 (over y, core).
Axes of the slice: x: 2, y: 2, z: 4, core: 2. Of those that a mesh axis runs over, the one named last changes fastest.
Arguments:
- tokens: bfloat16 [32768, 768], P(('dp', 'tensor')), may hold values from -6 to 6
- lengths: int32 [32], P('dp'), may hold values from 256 to 1024, as said below
- w_query: bfloat16 [768, 768], P('dp', 'tensor'), may hold values from -0.3125 to 0.3125
- w_key: bfloat16 [768, 768], P('dp', 'tensor'), may hold values from -0.3125 to 0.3125
- w_value: bfloat16 [768, 768], P('dp', 'tensor'), may hold values from -0.21875 to 0.21875
- w_out: bfloat16 [768, 768], P('tensor', 'dp'), may hold values from -1 to 1
- w_up: bfloat16 [768, 3072], P('dp', 'tensor'), may hold values from -0.21875 to 0.21875
- w_down: bfloat16 [3072, 768], P('tensor', 'dp'), may hold values from -0.109375 to 0.109375
- query_bias: float32 [768], P(('dp', 'tensor')), may hold values from -1.8 to 1.8
- value_bias: float32 [768], P(('dp', 'tensor')), may hold values from -1.8 to 1.8
- out_bias: float32 [768], P(('dp', 'tensor')), may hold values from -1.2 to 1.2
- attn_gain: float32 [768], P(('dp', 'tensor')), may hold values from 0.25 to 1.75
- attn_shift: float32 [768], P(('dp', 'tensor')), may hold values from -1.2 to 1.2
- up_bias: float32 [3072], P(('dp', 'tensor')), may hold values from -1.8 to 1.8
- down_bias: float32 [768], P(('dp', 'tensor')), may hold values from -1.2 to 1.2
- ffn_gain: float32 [768], P(('dp', 'tensor')), may hold values from 0.25 to 1.75
- ffn_shift: float32 [768], P(('dp', 'tensor')), may hold values from -1.8 to 1.8
- cotangent: bfloat16 [32768, 768], P(('dp', 'tensor')), may hold values from -6 to 6
Outputs:
- output: float32 [32768, 768], P(('dp', 'tensor'))
- grad_tokens: float32 [32768, 768], P(('dp', 'tensor'))
- query_grad: float32 [768, 768], P('dp', 'tensor')
- key_grad: float32 [768, 768], P('dp', 'tensor')
- value_grad: float32 [768, 768], P('dp', 'tensor')
- out_grad: float32 [768, 768], P('tensor', 'dp')
- up_grad: float32 [768, 3072], P('dp', 'tensor')
- down_grad: float32 [3072, 768], P('tensor', 'dp')
- query_bias_grad: float32 [768], P(('dp', 'tensor'))
- value_bias_grad: float32 [768], P(('dp', 'tensor'))
- out_bias_grad: float32 [768], P(('dp', 'tensor'))
- attn_gain_grad: float32 [768], P(('dp', 'tensor'))
- attn_shift_grad: float32 [768], P(('dp', 'tensor'))
- up_bias_grad: float32 [3072], P(('dp', 'tensor'))
- down_bias_grad: float32 [768], P(('dp', 'tensor'))
- ffn_gain_grad: float32 [768], P(('dp', 'tensor'))
- ffn_shift_grad: float32 [768], P(('dp', 'tensor'))
Inputs may be any that keep to these rules, and one draw needn't show every extreme that they name: `lengths`: each sequence's count of valid tokens, which come first in it; in every draw some sequence has all 1024 slots valid and some has 256.
All inputs are finite; a program needn't handle non-finite values.
Results may differ from a plain program's by a relative error of at most 0.019.
Values may be sent and summed in bfloat16 or wider, within the bound.
A program may use at most 192 MiB of HBM per device.

v0:
```python
import jax
import jax.numpy as jnp
from jax import lax
from jax.sharding import PartitionSpec as P

HEAD = 64


EPSILON = 1e-12
FLOOR_SCORE = -1e30


def cut_along(shard, dim, peers):
    before, after = (shard.shape[:dim], shard.shape[dim + 1 :])
    return jnp.moveaxis(shard.reshape(*before, peers, -1, *after), dim, 0)


def sum_at_owner(shard, axis, dim):
    parts = cut_along(shard, dim, lax.axis_size(axis))
    arrived = lax.all_to_all(parts, axis, split_axis=0, concat_axis=0, tiled=True)
    return arrived.astype(jnp.float32).sum(axis=0)


def side_by_side(arrays, axis, dim, along):
    widths = [a.shape[along] for a in arrays]
    both = jnp.concatenate(arrays, axis=along)
    whole = sum_at_owner(both, axis, dim)
    return tuple(jnp.split(whole, [sum(widths[:k]) for k in range(1, len(widths))], axis=along))


def matmul(left_side, right_side):
    return jnp.dot(left_side, right_side, preferred_element_type=jnp.float32)


def contract_rows(left_side, right_side):
    return lax.dot_general(
        left_side, right_side, (((0,), (0,)), ((), ())), preferred_element_type=jnp.float32
    )


def contract_cols(left_side, right_side):
    return lax.dot_general(
        left_side, right_side, (((1,), (1,)), ((), ())), preferred_element_type=jnp.float32
    )


def round_trip(operand):
    return lax.optimization_barrier(operand.astype(jnp.bfloat16)).astype(jnp.float32)


def layer_norm(values, norm_gain, norm_shift):
    center = values - jnp.mean(values, axis=-1, keepdims=True)
    spread = jnp.mean(center * center, axis=-1, keepdims=True)
    return center * lax.rsqrt(spread + EPSILON) * norm_gain + norm_shift


def gelu_exact(values):
    return jax.nn.gelu(values, approximate=False)


def head_scores(query_seq, key_seq, length):
    scores = jnp.einsum(
        "qhd,khd->hqk", query_seq, key_seq, preferred_element_type=jnp.float32
    ) * HEAD ** (-0.5)
    counted = jnp.arange(key_seq.shape[0], dtype=jnp.int32) < length
    return (jnp.where(counted[None, None, :], scores, FLOOR_SCORE), counted)


def attend_forward(seq_items):
    query_seq, key_seq, value_seq, length = seq_items
    scores, counted = head_scores(query_seq, key_seq, length)
    row_top = jnp.max(scores, axis=-1, keepdims=True)
    exp_terms = jnp.exp(scores - row_top)
    row_total = jnp.sum(exp_terms, axis=-1, keepdims=True)
    prob_low = (exp_terms / row_total).astype(jnp.bfloat16)
    head_mix = jnp.einsum("hqk,khd->qhd", prob_low, value_seq, preferred_element_type=jnp.float32)
    return (head_mix.astype(jnp.bfloat16), (row_top + jnp.log(row_total))[..., 0])


def attend_backward(seq_items):
    query_seq, key_seq, value_seq, length, log_total, grad_mix = seq_items
    scores, counted = head_scores(query_seq, key_seq, length)
    prob_full = jnp.exp(scores - log_total[..., None])
    prob_low = prob_full.astype(jnp.bfloat16)
    grad_value = jnp.einsum("hqk,qhd->khd", prob_low, grad_mix, preferred_element_type=jnp.float32)
    grad_probs = jnp.einsum("qhd,khd->hqk", grad_mix, value_seq, preferred_element_type=jnp.float32)
    row_inner = jnp.sum(prob_full * grad_probs, axis=-1, keepdims=True)
    grad_scores = jnp.where(
        counted[None, None, :], prob_full * (grad_probs - row_inner), 0.0
    ).astype(jnp.bfloat16)
    score_scale = HEAD ** (-0.5)
    grad_query = (
        jnp.einsum("hqk,khd->qhd", grad_scores, key_seq, preferred_element_type=jnp.float32)
        * score_scale
    )
    grad_key = (
        jnp.einsum("hqk,qhd->khd", grad_scores, query_seq, preferred_element_type=jnp.float32)
        * score_scale
    )
    return (
        grad_query.astype(jnp.bfloat16),
        grad_key.astype(jnp.bfloat16),
        grad_value.astype(jnp.bfloat16),
    )


def shards(
    tokens,
    lengths,
    w_query,
    w_key,
    w_value,
    w_out,
    w_up,
    w_down,
    query_bias,
    value_bias,
    out_bias,
    attn_gain,
    attn_shift,
    up_bias,
    down_bias,
    ffn_gain,
    ffn_shift,
    cotangent,
):
    tensor_rank = lax.axis_index("tensor")
    small_full = (
        lax.all_gather(query_bias, ("dp", "tensor"), axis=0, tiled=True),
        lax.all_gather(value_bias, ("dp", "tensor"), axis=0, tiled=True),
        lax.all_gather(out_bias, ("dp", "tensor"), axis=0, tiled=True),
        lax.all_gather(attn_gain, ("dp", "tensor"), axis=0, tiled=True),
        lax.all_gather(attn_shift, ("dp", "tensor"), axis=0, tiled=True),
        lax.all_gather(up_bias, ("dp", "tensor"), axis=0, tiled=True),
        lax.all_gather(down_bias, ("dp", "tensor"), axis=0, tiled=True),
        lax.all_gather(ffn_gain, ("dp", "tensor"), axis=0, tiled=True),
        lax.all_gather(ffn_shift, ("dp", "tensor"), axis=0, tiled=True),
    )
    (
        qbias_full,
        vbias_full,
        obias_full,
        gain_one,
        shift_one,
        ubias_full,
        dbias_full,
        gain_two,
        shift_two,
    ) = small_full
    query_weight, key_weight, value_weight, out_weight, up_weight, down_weight = (
        lax.all_gather(w_query, "dp", axis=0, tiled=True),
        lax.all_gather(w_key, "dp", axis=0, tiled=True),
        lax.all_gather(w_value, "dp", axis=0, tiled=True),
        lax.all_gather(w_out, "dp", axis=1, tiled=True),
        lax.all_gather(w_up, "dp", axis=0, tiled=True),
        lax.all_gather(w_down, "dp", axis=1, tiled=True),
    )
    row_count = tokens.shape[0]
    model_width = tokens.shape[1]
    head_cols = query_weight.shape[1]
    local_heads = head_cols // HEAD
    seq_count = lengths.shape[0]
    group_total = row_count * lax.axis_size("tensor")
    seq_len = group_total // seq_count
    head_offset = tensor_rank * head_cols

    def to_heads(matrix):
        return matrix.reshape(seq_count, seq_len, local_heads, HEAD)

    group_rows = lax.all_gather(tokens, "tensor", axis=0, tiled=True)
    query_shift = lax.dynamic_slice_in_dim(qbias_full, head_offset, head_cols)
    value_shift = lax.dynamic_slice_in_dim(vbias_full, head_offset, head_cols)
    queries = (matmul(group_rows, query_weight) + query_shift).astype(jnp.bfloat16)
    keys_low = matmul(group_rows, key_weight).astype(jnp.bfloat16)
    values_low = (matmul(group_rows, value_weight) + value_shift).astype(jnp.bfloat16)
    head_mix, log_totals = lax.map(
        attend_forward, (to_heads(queries), to_heads(keys_low), to_heads(values_low), lengths)
    )
    mixed_rows = head_mix.reshape(group_total, head_cols)
    attention = (
        lax.psum_scatter(
            matmul(mixed_rows, out_weight).astype(jnp.bfloat16),
            "tensor",
            scatter_dimension=0,
            tiled=True,
        ).astype(jnp.float32)
        + obias_full
    )
    residual_one = tokens.astype(jnp.float32) + attention
    hidden, norm_one_back = jax.vjp(layer_norm, residual_one, gain_one, shift_one)
    hidden_low = hidden.astype(jnp.bfloat16)
    unit_cols = up_weight.shape[1]
    ffn_rows = lax.all_gather(hidden_low, "tensor", axis=0, tiled=True)
    up_shift = lax.dynamic_slice_in_dim(ubias_full, tensor_rank * unit_cols, unit_cols)
    pre_act = matmul(ffn_rows, up_weight) + up_shift
    act_full, gelu_back = jax.vjp(gelu_exact, pre_act)
    act_low = act_full.astype(jnp.bfloat16)
    branch = (
        lax.psum_scatter(
            matmul(act_low, down_weight).astype(jnp.bfloat16),
            "tensor",
            scatter_dimension=0,
            tiled=True,
        ).astype(jnp.float32)
        + dbias_full
    )
    residual_two = hidden + branch
    normed, norm_two_back = jax.vjp(layer_norm, residual_two, gain_two, shift_two)
    positions = tensor_rank * row_count + jnp.arange(row_count, dtype=jnp.int32)
    seq_of_row = positions // seq_len
    row_length = jnp.sum(
        jnp.where(
            seq_of_row[:, None] == jnp.arange(seq_count, dtype=jnp.int32)[None, :],
            lengths[None, :],
            0,
        ),
        axis=1,
    )
    valid = (positions % seq_len < row_length).astype(jnp.float32)[:, None]
    output = normed * valid
    grad_second, ffn_gain_grad, ffn_shift_grad = norm_two_back(
        cotangent.astype(jnp.float32) * valid
    )
    grad_branch = grad_second.astype(jnp.bfloat16)
    down_bias_grad = jnp.sum(grad_branch.astype(jnp.float32), axis=0)
    branch_rows = lax.all_gather(grad_branch, "tensor", axis=0, tiled=True)
    grad_act = contract_cols(branch_rows, down_weight).astype(jnp.bfloat16)
    down_grad = contract_rows(act_low, branch_rows)
    grad_pre = gelu_back(grad_act.astype(jnp.float32))[0].astype(jnp.bfloat16)
    up_grad = contract_rows(ffn_rows, grad_pre)
    up_part = jnp.sum(grad_pre.astype(jnp.float32), axis=0)
    up_bias_grad = lax.dynamic_update_slice_in_dim(
        jnp.zeros(ubias_full.shape, jnp.float32), up_part, tensor_rank * unit_cols, 0
    )
    grad_from_ffn = lax.psum_scatter(
        contract_cols(grad_pre, up_weight).astype(jnp.bfloat16),
        "tensor",
        scatter_dimension=0,
        tiled=True,
    ).astype(jnp.float32)
    grad_hidden = grad_second + round_trip(grad_from_ffn)
    grad_first, attn_gain_grad, attn_shift_grad = norm_one_back(grad_hidden)
    grad_attn = grad_first.astype(jnp.bfloat16)
    out_bias_grad = jnp.sum(grad_attn.astype(jnp.float32), axis=0)
    attn_grad_rows = lax.all_gather(grad_attn, "tensor", axis=0, tiled=True)
    grad_mixed = contract_cols(attn_grad_rows, out_weight).astype(jnp.bfloat16)
    out_grad = contract_rows(mixed_rows, attn_grad_rows)
    grad_queries, grad_keys, grad_values = lax.map(
        attend_backward,
        (
            to_heads(queries),
            to_heads(keys_low),
            to_heads(values_low),
            lengths,
            log_totals,
            to_heads(grad_mixed),
        ),
    )
    grad_queries = grad_queries.reshape(group_total, head_cols)
    grad_keys = grad_keys.reshape(group_total, head_cols)
    grad_values = grad_values.reshape(group_total, head_cols)
    query_grad = contract_rows(group_rows, grad_queries)
    key_grad = contract_rows(group_rows, grad_keys)
    value_grad = contract_rows(group_rows, grad_values)
    blank_width = jnp.zeros((model_width,), jnp.float32)
    query_bias_grad = lax.dynamic_update_slice_in_dim(
        blank_width, jnp.sum(grad_queries.astype(jnp.float32), axis=0), head_offset, 0
    )
    value_bias_grad = lax.dynamic_update_slice_in_dim(
        blank_width, jnp.sum(grad_values.astype(jnp.float32), axis=0), head_offset, 0
    )
    input_part = (
        contract_cols(grad_queries, query_weight)
        + contract_cols(grad_keys, key_weight)
        + contract_cols(grad_values, value_weight)
    )
    grad_tokens = grad_first + lax.psum_scatter(
        input_part.astype(jnp.bfloat16), "tensor", scatter_dimension=0, tiled=True
    ).astype(jnp.float32)
    owned = (
        *side_by_side(
            (
                query_grad.astype(jnp.bfloat16),
                key_grad.astype(jnp.bfloat16),
                value_grad.astype(jnp.bfloat16),
            ),
            "dp",
            0,
            1,
        ),
        sum_at_owner(out_grad.astype(jnp.bfloat16), "dp", 1),
        sum_at_owner(up_grad.astype(jnp.bfloat16), "dp", 0),
        sum_at_owner(down_grad.astype(jnp.bfloat16), "dp", 1),
    )
    small_owned = (
        lax.psum_scatter(query_bias_grad, ("dp", "tensor"), scatter_dimension=0, tiled=True),
        lax.psum_scatter(value_bias_grad, ("dp", "tensor"), scatter_dimension=0, tiled=True),
        lax.psum_scatter(out_bias_grad, ("dp", "tensor"), scatter_dimension=0, tiled=True),
        lax.psum_scatter(attn_gain_grad, ("dp", "tensor"), scatter_dimension=0, tiled=True),
        lax.psum_scatter(attn_shift_grad, ("dp", "tensor"), scatter_dimension=0, tiled=True),
        lax.psum_scatter(up_bias_grad, ("dp", "tensor"), scatter_dimension=0, tiled=True),
        lax.psum_scatter(down_bias_grad, ("dp", "tensor"), scatter_dimension=0, tiled=True),
        lax.psum_scatter(ffn_gain_grad, ("dp", "tensor"), scatter_dimension=0, tiled=True),
        lax.psum_scatter(ffn_shift_grad, ("dp", "tensor"), scatter_dimension=0, tiled=True),
    )
    return (
        output,
        grad_tokens,
        owned[0],
        owned[1],
        owned[2],
        owned[3],
        owned[4],
        owned[5],
        small_owned[0],
        small_owned[1],
        small_owned[2],
        small_owned[3],
        small_owned[4],
        small_owned[5],
        small_owned[6],
        small_owned[7],
        small_owned[8],
    )


def solution(mesh):
    placed = (
        P(("dp", "tensor"), None),
        P("dp"),
        P("dp", "tensor"),
        P("dp", "tensor"),
        P("dp", "tensor"),
        P("tensor", "dp"),
        P("dp", "tensor"),
        P("tensor", "dp"),
        P(("dp", "tensor")),
        P(("dp", "tensor")),
        P(("dp", "tensor")),
        P(("dp", "tensor")),
        P(("dp", "tensor")),
        P(("dp", "tensor")),
        P(("dp", "tensor")),
        P(("dp", "tensor")),
        P(("dp", "tensor")),
        P(("dp", "tensor"), None),
    )
    return jax.shard_map(
        shards,
        mesh=mesh,
        in_specs=placed,
        out_specs=(
            P(("dp", "tensor"), None),
            P(("dp", "tensor"), None),
            P("dp", "tensor"),
            P("dp", "tensor"),
            P("dp", "tensor"),
            P("tensor", "dp"),
            P("dp", "tensor"),
            P("tensor", "dp"),
            P(("dp", "tensor")),
            P(("dp", "tensor")),
            P(("dp", "tensor")),
            P(("dp", "tensor")),
            P(("dp", "tensor")),
            P(("dp", "tensor")),
            P(("dp", "tensor")),
            P(("dp", "tensor")),
            P(("dp", "tensor")),
        ),
        check_vma=False,
    )
```

profile of v0, /device:TPU:0, one launch (start us, length us, event | category | flops | bytes accessed | tf_op | source)
XLA Modules:
  0.0 1138.1 jit_solution(15248481869915932841)
XLA Ops:
  15.5 44.0 %all-reduce.19 = (f32[768]{0:T(1024)}, f32[768]{0:T(1024)}, f32[768]{0:T(1024)S(1)}, f32[768]{0:T(1024)S(1)}, f32[768]{0:T(1024)S(1)}, /*index=5*/f32[3072]{0:T(1024)}, f32[768]{0:T(1024)}, f32[768]{0:T(1024)}) all-reduce(f32[768]{0:T(1024)S(1)} %dynamic-update-slice.4, ...), channel_id=1, replica_groups=mesh['dp'=8,'tensor'=4] {'dp','tensor'}, use_global_device_ids=true, to_apply=%add.4 | all-reduce | flops 8448 | bytes 67584
  60.6 31.0 %all_gather.63 = bf16[192,768]{0,1:T(8,128)(2,1)S(1)} all-gather(bf16[192,96]{0,1:T(8,128)(2,1)S(1)} %copy.88), channel_id=1, replica_groups=mesh['dp'=8,'tensor'=4] {'dp'}, dimensions={1}, use_global_device_ids=true | all-gather | bytes 331776 | tf_op jit(solution)/shard_map/all_gather | solution.py:154
  91.5 33.2 %all_gather.60 = bf16[768,192]{1,0:T(8,128)(2,1)} all-gather(bf16[96,192]{1,0:T(8,128)(2,1)} %param.24), channel_id=1, replica_groups=mesh['dp'=8,'tensor'=4] {'dp'}, dimensions={0}, use_global_device_ids=true | all-gather | bytes 331776 | tf_op jit(solution)/shard_map/all_gather | solution.py:151
  124.7 33.3 %all_gather.62 = bf16[768,192]{1,0:T(8,128)(2,1)} all-gather(bf16[96,192]{1,0:T(8,128)(2,1)} %param.25), channel_id=1, replica_groups=mesh['dp'=8,'tensor'=4] {'dp'}, dimensions={0}, use_global_device_ids=true | all-gather | bytes 331776 | tf_op jit(solution)/shard_map/all_gather | solution.py:152
  158.0 31.2 %all_gather.58 = bf16[768,192]{1,0:T(8,128)(2,1)S(1)} all-gather(bf16[96,192]{1,0:T(8,128)(2,1)S(1)} %copy-done.42), channel_id=1, replica_groups=mesh['dp'=8,'tensor'=4] {'dp'}, dimensions={0}, use_global_device_ids=true | all-gather | bytes 331776 | tf_op jit(solution)/shard_map/all_gather | solution.py:153
  215.6 49.6 %while.26 = (s32[]{:T(128)}, bf16[4,1024,3,64]{1,3,2,0:T(8,128)(2,1)}, f32[4,3,1024]{2,1,0:T(4,128)}, bf16[4,1024,3,64]{1,3,2,0:T(8,128)(2,1)}, s32[4]{0:T(128)S...) while((s32[]{:T(128)}, ...), condition=%wide.region_3.4_spmd, body=%wide.region_0.3_spmd.sunk | while | flops 843249664 | bytes 39430256 | solution.py:176
  276.3 58.1 %reduce-scatter.5.cloned.1.call-done = bf16[1024,768]{1,0:T(8,128)(2,1)} async-done(((bf16[4096,768]{1,0:T(8,128)(2,1)}), bf16[1024,768]{1,0:T(8,128)(2,1)}) %reduce-scatter.5.cloned.1.call-update) | async-done | bytes 1572880 | tf_op jit(solution)/shard_map/reduce_scatter | solution.py:181
  340.9 44.9 %all-gather.9.cloned.1.call-done = bf16[4096,768]{1,0:T(8,128)(2,1)} async-done(((bf16[1024,768]{1,0:T(8,128)(2,1)}), bf16[4096,768]{1,0:T(8,128)(2,1)}) %all-gather.9.cloned.1.call-update) | async-done | bytes 6291472 | tf_op jit(solution)/shard_map/all_gather | solution.py:193
  385.9 34.8 %multiply_convert_fusion = (bf16[4096,768]{1,0:T(8,128)(2,1)}, f32[4096,768]{1,0:T(8,128)}, f32[4096,768]{1,0:T(8,128)}) fusion(f32[768]{0:T(1024)S(1)} %dynamic_slice.44, bf16[4096,768]{1,0:T(8,128)(2,1)} %all-gather.9.cloned.1.call-done, bf16[768,768]{1,0:T(8,128)(2,1)} %all-gather.11.cloned.1.call-done), kind=kOutput, calls=%fused_computation.97 | convolution fusion | flops 5039456256 | bytes 38931456 | tf_op jit(solution)/shard_map/dot_general | solution.py:32
  420.7 8.6 all-gather.13.cloned.1.call-done
  429.3 9.2 convolution_convert_fusion.3
  438.9 56.9 %reduce-scatter.7.cloned.1.call-done = bf16[1024,768]{1,0:T(8,128)(2,1)} async-done(((bf16[4096,768]{1,0:T(8,128)(2,1)}), bf16[1024,768]{1,0:T(8,128)(2,1)}) %reduce-scatter.7.cloned.1.call-update) | async-done | bytes 1572880 | tf_op jit(solution)/shard_map/reduce_scatter | solution.py:199
  509.1 46.5 %all-gather.15.cloned.1.call-done = bf16[4096,768]{1,0:T(8,128)(2,1)} async-done(((bf16[1024,768]{1,0:T(8,128)(2,1)}), bf16[4096,768]{1,0:T(8,128)(2,1)}) %all-gather.15.cloned.1.call-update) | async-done | bytes 6291472 | tf_op jit(solution)/shard_map/all_gather | solution.py:226
  555.6 19.1 %convert_reduce_fusion = (f32[768]{0:T(1024)}, bf16[4096,768]{1,0:T(8,128)(2,1)}) fusion(f32[4096,768]{1,0:T(8,128)} %get-tuple-element.253, f32[4096,768]{1,0:T(8,128)} %get-tuple-element.259, f32[768]{0:T(1024)S(1)} %dynamic_slice.44, bf16[4096,768]{1,0:T(8,128)(2,1)} %all-gather.15.cloned.1.call-done, bf16[768,768]{0,1:T(8,128)(2,1)} %all-gather.13.cloned.1.call-done), kind=kOutput, calls=%fused_computation.95 | convolution fusion | flops 4891606016 | bytes 38934528 | tf_op jit(solution)/shard_map/dot_general | solution.py:42
  574.6 9.7 convolution_convert_fusion.1
  584.4 58.8 %reduce-scatter.9.cloned.1.call-done = bf16[1024,768]{1,0:T(8,128)(2,1)} async-done(((bf16[4096,768]{1,0:T(8,128)(2,1)}), bf16[1024,768]{1,0:T(8,128)(2,1)}) %reduce-scatter.9.cloned.1.call-update) | async-done | bytes 1572880 | tf_op jit(solution)/shard_map/reduce_scatter | solution.py:235
  653.9 46.5 %all-gather.17.cloned.1.call-done = bf16[4096,768]{1,0:T(8,128)(2,1)} async-done(((bf16[1024,768]{1,0:T(8,128)(2,1)}), bf16[4096,768]{1,0:T(8,128)(2,1)}) %all-gather.17.cloned.1.call-update) | async-done | bytes 6291472 | tf_op jit(solution)/shard_map/all_gather | solution.py:245
  712.4 220.9 %while.27 = (s32[]{:T(128)}, bf16[4,1024,3,64]{1,3,2,0:T(8,128)(2,1)}, bf16[4,1024,3,64]{1,3,2,0:T(8,128)(2,1)}, bf16[4,1024,3,64]{1,3,2,0:T(8,128)(2,1)}, bf16[...) while((s32[]{:T(128)}, ...), condition=%wide.region_18.19_spmd, body=%wide.region_16.18_spmd.sunk | while | flops 2096047104 | bytes 199085264 | solution.py:248
  728.6 19.8 %fusion.228 = bf16[4,1024,3,64]{1,3,2,0:T(8,128)(2,1)} fusion(bf16[4,1024,3,64]{1,3,2,0:T(8,128)(2,1)} %get-tuple-element.407, s32[]{:T(128)S(6)} %copy.135, f32[3,1024,1024]{1,2,0:T(8,128)} %fusion.225, f32[3,1024,1024]{1,2,0:T(8,128)} %copy-done, f32[3,1024]{1,0:T(4,128)S(1)} %dynamic-slice_bitcast_fusion.2, ...), kind=kOutput, calls=%fused_computation.52.clone.1 | convolution fusion | flops 437653504 | bytes 51153920 | tf_op jit(solution)/shard_map/while/body/eval_jaxpr/hqk,qhd->khd/dot_general | solution.py:97
  748.4 19.5 %fusion.227 = bf16[4,1024,3,64]{1,3,2,0:T(8,128)(2,1)} fusion(bf16[4,1024,3,64]{1,3,2,0:T(8,128)(2,1)} %get-tuple-element.406, s32[]{:T(128)S(6)} %copy.135, f32[3,1024,1024]{1,2,0:T(8,128)} %fusion.225, f32[3,1024,1024]{1,2,0:T(8,128)} %copy-done, f32[3,1024]{1,0:T(4,128)S(1)} %dynamic-slice_bitcast_fusion.2, ...), kind=kOutput, calls=%fused_computation.50.clone.1 | convolution fusion | flops 437653504 | bytes 51153920 | tf_op jit(solution)/shard_map/while/body/eval_jaxpr/hqk,khd->qhd/dot_general | solution.py:93
  783.7 19.8 %fusion.228 = bf16[4,1024,3,64]{1,3,2,0:T(8,128)(2,1)} fusion(bf16[4,1024,3,64]{1,3,2,0:T(8,128)(2,1)} %get-tuple-element.407, s32[]{:T(128)S(6)} %copy.135, f32[3,1024,1024]{1,2,0:T(8,128)} %fusion.225, f32[3,1024,1024]{1,2,0:T(8,128)} %copy-done, f32[3,1024]{1,0:T(4,128)S(1)} %dynamic-slice_bitcast_fusion.2, ...), kind=kOutput, calls=%fused_computation.52.clone.1 | convolution fusion | flops 437653504 | bytes 51153920 | tf_op jit(solution)/shard_map/while/body/eval_jaxpr/hqk,qhd->khd/dot_general | solution.py:97
  803.5 19.5 %fusion.227 = bf16[4,1024,3,64]{1,3,2,0:T(8,128)(2,1)} fusion(bf16[4,1024,3,64]{1,3,2,0:T(8,128)(2,1)} %get-tuple-element.406, s32[]{:T(128)S(6)} %copy.135, f32[3,1024,1024]{1,2,0:T(8,128)} %fusion.225, f32[3,1024,1024]{1,2,0:T(8,128)} %copy-done, f32[3,1024]{1,0:T(4,128)S(1)} %dynamic-slice_bitcast_fusion.2, ...), kind=kOutput, calls=%fused_computation.50.clone.1 | convolution fusion | flops 437653504 | bytes 51153920 | tf_op jit(solution)/shard_map/while/body/eval_jaxpr/hqk,khd->qhd/dot_general | solution.py:93
  838.8 19.8 %fusion.228 = bf16[4,1024,3,64]{1,3,2,0:T(8,128)(2,1)} fusion(bf16[4,1024,3,64]{1,3,2,0:T(8,128)(2,1)} %get-tuple-element.407, s32[]{:T(128)S(6)} %copy.135, f32[3,1024,1024]{1,2,0:T(8,128)} %fusion.225, f32[3,1024,1024]{1,2,0:T(8,128)} %copy-done, f32[3,1024]{1,0:T(4,128)S(1)} %dynamic-slice_bitcast_fusion.2, ...), kind=kOutput, calls=%fused_computation.52.clone.1 | convolution fusion | flops 437653504 | bytes 51153920 | tf_op jit(solution)/shard_map/while/body/eval_jaxpr/hqk,qhd->khd/dot_general | solution.py:97
  858.6 19.5 %fusion.227 = bf16[4,1024,3,64]{1,3,2,0:T(8,128)(2,1)} fusion(bf16[4,1024,3,64]{1,3,2,0:T(8,128)(2,1)} %get-tuple-element.406, s32[]{:T(128)S(6)} %copy.135, f32[3,1024,1024]{1,2,0:T(8,128)} %fusion.225, f32[3,1024,1024]{1,2,0:T(8,128)} %copy-done, f32[3,1024]{1,0:T(4,128)S(1)} %dynamic-slice_bitcast_fusion.2, ...), kind=kOutput, calls=%fused_computation.50.clone.1 | convolution fusion | flops 437653504 | bytes 51153920 | tf_op jit(solution)/shard_map/while/body/eval_jaxpr/hqk,khd->qhd/dot_general | solution.py:93
  893.9 19.8 %fusion.228 = bf16[4,1024,3,64]{1,3,2,0:T(8,128)(2,1)} fusion(bf16[4,1024,3,64]{1,3,2,0:T(8,128)(2,1)} %get-tuple-element.407, s32[]{:T(128)S(6)} %copy.135, f32[3,1024,1024]{1,2,0:T(8,128)} %fusion.225, f32[3,1024,1024]{1,2,0:T(8,128)} %copy-done, f32[3,1024]{1,0:T(4,128)S(1)} %dynamic-slice_bitcast_fusion.2, ...), kind=kOutput, calls=%fused_computation.52.clone.1 | convolution fusion | flops 437653504 | bytes 51153920 | tf_op jit(solution)/shard_map/while/body/eval_jaxpr/hqk,qhd->khd/dot_general | solution.py:97
  913.7 19.5 %fusion.227 = bf16[4,1024,3,64]{1,3,2,0:T(8,128)(2,1)} fusion(bf16[4,1024,3,64]{1,3,2,0:T(8,128)(2,1)} %get-tuple-element.406, s32[]{:T(128)S(6)} %copy.135, f32[3,1024,1024]{1,2,0:T(8,128)} %fusion.225, f32[3,1024,1024]{1,2,0:T(8,128)} %copy-done, f32[3,1024]{1,0:T(4,128)S(1)} %dynamic-slice_bitcast_fusion.2, ...), kind=kOutput, calls=%fused_computation.50.clone.1 | convolution fusion | flops 437653504 | bytes 51153920 | tf_op jit(solution)/shard_map/while/body/eval_jaxpr/hqk,khd->qhd/dot_general | solution.py:93
  955.3 12.1 %add_convert_fusion = bf16[4096,768]{1,0:T(8,128)(2,1)} fusion(f32[4096,768]{1,0:T(8,128)} %fusion.154, f32[4096,768]{1,0:T(8,128)} %fusion.155, bf16[4096,192]{0,1:T(8,128)(2,1)S(1)} %bitcast.183, bf16[768,192]{1,0:T(8,128)(2,1)S(1)} %copy-done.28), kind=kOutput, calls=%fused_computation.96 | convolution fusion | flops 1217396736 | bytes 33325056 | tf_op jit(solution)/shard_map/dot_general | solution.py:42
  967.4 10.1 convolution_convert_fusion.6
  983.0 9.8 convolution_convert_fusion.7
  992.9 19.1 %all-to-all-done.3 = bf16[8,768,96]{1,2,0:T(8,128)(2,1)S(1)} async-done(((bf16[8,768,96]{1,2,0:T(8,128)(2,1)}), bf16[8,768,96]{1,2,0:T(8,128)(2,1)S(1)}, u32[]{:S(2)}, u32[]{:S(2)}) %all-to-all-start.3) | async-done | bytes 1179680 | tf_op jit(solution)/shard_map/all_to_all | solution.py:20
  1034.1 11.3 all-to-all-done.2
  1074.5 41.1 %all-reduce.18 = (f32[768]{0:T(1024)S(1)}, f32[768]{0:T(1024)S(1)}, f32[768]{0:T(1024)S(1)}, f32[768]{0:T(1024)S(1)}, f32[768]{0:T(1024)S(1)}, /*index=5*/f32[76...) all-reduce(f32[768]{0:T(1024)S(1)} %dynamic-update-slice.8, ...), channel_id=1, replica_groups=mesh['dp'=8,'tensor'=4] {'dp','tensor'}, use_global_device_ids=true, to_apply=%add.8 | all-reduce | flops 9984 | bytes 79872
  (321 shorter events, 294.3 us)
Async XLA Ops:
  8.0 150.0 %copy-start.42 = (bf16[96,192]{1,0:T(8,128)(2,1)S(1)}, bf16[96,192]{1,0:T(8,128)(2,1)}, u32[]{:S(2)}) copy-start(bf16[96,192]{1,0:T(8,128)(2,1)} %param.26) | copy-start | bytes 110596
  8.0 181.2 %all-gather.7.cloned.1.call-start = ((), (), s32[]{:S(2)}) async-start(), calls=%async_computation.8 | async-start | bytes 7864320 | tf_op jit(solution)/shard_map/all_gather | solution.py:170
  8.8 325.7 %reduce-scatter.5.cloned.1.call-start = ((), (), s32[]{:S(2)}) async-start(), calls=%async_computation.9 | async-start | bytes 7864320 | tf_op jit(solution)/shard_map/reduce_scatter | solution.py:181
  91.5 178.1 %copy-start.23 = (bf16[192,768]{0,1:T(8,128)(2,1)}, bf16[192,768]{0,1:T(8,128)(2,1)S(1)}, u32[]{:S(2)}) copy-start(bf16[192,768]{0,1:T(8,128)(2,1)S(1)} %all_gather.63) | copy-start | bytes 884740
  275.3 59.2 %copy-start.3 = (bf16[1024,768]{1,0:T(8,128)(2,1)S(1)}, bf16[1024,768]{1,0:T(8,128)(2,1)}, u32[]{:S(2)}) copy-start(bf16[1024,768]{1,0:T(8,128)(2,1)} %param.22) | copy-start | bytes 4718596
  275.3 65.6 %all-gather.11.cloned.1.call-start = ((), (), s32[]{:S(2)}) async-start(), calls=%async_computation.11 | async-start | bytes 1327104 | tf_op jit(solution)/shard_map/all_gather | solution.py:155
  275.9 110.0 %all-gather.9.cloned.1.call-start = ((), (), s32[]{:S(2)}) async-start(), calls=%async_computation.10 | async-start | bytes 7864320 | tf_op jit(solution)/shard_map/all_gather | solution.py:193
  339.5 89.8 %all-gather.13.cloned.1.call-start = ((), (), s32[]{:S(2)}) async-start(), calls=%async_computation.12 | async-start | bytes 1327104 | tf_op jit(solution)/shard_map/all_gather | solution.py:156
  340.1 155.7 %reduce-scatter.7.cloned.1.call-start = ((), (), s32[]{:S(2)}) async-start(), calls=%async_computation.13 | async-start | bytes 7864320 | tf_op jit(solution)/shard_map/reduce_scatter | solution.py:199
  438.5 57.3 %copy-start.56 = (f32[768]{0:T(1024)S(1)}, f32[768]{0:T(1024)}, u32[]{:S(2)}) copy-start(f32[768]{0:T(1024)} %get-tuple-element.238) | copy-start | bytes 9220
  438.5 117.0 %all-gather.15.cloned.1.call-start = ((), (), s32[]{:S(2)}) async-start(), calls=%async_computation.14 | async-start | bytes 7864320 | tf_op jit(solution)/shard_map/all_gather | solution.py:226
  438.9 64.6 %copy-start.38 = (f32[1024]{0:T(1024)}, f32[1024]{0:T(1024)S(1)}, u32[]{:S(2)}) copy-start(f32[1024]{0:T(1024)S(1)} %fusion.144) | copy-start | bytes 12292
  509.0 134.2 %reduce-scatter.9.cloned.1.call-start = ((), (), s32[]{:S(2)}) async-start(), calls=%async_computation.15 | async-start | bytes 7864320 | tf_op jit(solution)/shard_map/reduce_scatter | solution.py:235
  555.6 19.1 %copy-start.59 = (bf16[768,768]{1,0:T(8,128)(2,1)S(1)}, bf16[768,768]{1,0:T(8,128)(2,1)}, u32[]{:S(2)}) copy-start(bf16[768,768]{1,0:T(8,128)(2,1)} %all-gather.11.cloned.1.call-done) | copy-start | bytes 3538948
  584.4 63.5 %copy-start.46 = (f32[1024]{0:T(1024)S(1)}, f32[1024]{0:T(1024)}, u32[]{:S(2)}) copy-start(f32[1024]{0:T(1024)} %copy-done.45) | copy-start | bytes 12292
  584.4 116.0 %all-gather.17.cloned.1.call-start = ((), (), s32[]{:S(2)}) async-start(), calls=%async_computation.16 | async-start | bytes 7864320 | tf_op jit(solution)/shard_map/all_gather | solution.py:245
  651.8 48.6 %copy-start.24 = (bf16[192,768]{0,1:T(8,128)(2,1)S(1)}, bf16[192,768]{0,1:T(8,128)(2,1)}, u32[]{:S(2)}) copy-start(bf16[192,768]{0,1:T(8,128)(2,1)} %copy-done.23) | copy-start | bytes 884740
  653.9 472.3 %reduce-scatter.11.cloned.1.call-start = ((), (), s32[]{:S(2)}) async-start(), calls=%async_computation.17 | async-start | bytes 7864320 | tf_op jit(solution)/shard_map/reduce_scatter | solution.py:277
  938.6 10.3 copy-start.16
  942.4 12.9 %copy-start.18 = (bf16[24,8,4,1024]{3,1,2,0:T(8,128)(2,1)}, bf16[24,8,4,1024]{3,1,2,0:T(8,128)(2,1)S(1)}, u32[]{:S(2)}) copy-start(bf16[24,8,4,1024]{3,1,2,0:T(8,128)(2,1)S(1)} %copy.105) | copy-start | bytes 4718596
  977.5 34.5 %all-to-all-start.3 = ((bf16[8,768,96]{1,2,0:T(8,128)(2,1)}), bf16[8,768,96]{1,2,0:T(8,128)(2,1)S(1)}, u32[]{:S(2)}, u32[]{:S(2)}) async-start(bf16[8,768,96]{1,2,0:T(8,128)(2,1)} %bitcast.26), calls=%async_computation.7 | async-start | bytes 2359296 | tf_op jit(solution)/shard_map/all_to_all | solution.py:20
  1013.0 32.4 %all-to-all-start.2 = ((bf16[8,96,768]{2,1,0:T(8,128)(2,1)}), bf16[8,96,768]{2,1,0:T(8,128)(2,1)S(1)}, u32[]{:S(2)}, u32[]{:S(2)}) async-start(bf16[8,96,768]{2,1,0:T(8,128)(2,1)} %bitcast.190), calls=%async_computation.6 | async-start | bytes 2359296 | tf_op jit(solution)/shard_map/all_to_all | solution.py:20
  1016.7 15.3 %slice-start = ((s8[6291456]{0:T(1024)(128)(4,1)}), s8[2097152]{0:T(1024)(128)(4,1)S(1)}, s32[]{:S(2)}) async-start(s8[6291456]{0:T(1024)(128)(4,1)} %bitcast.175), calls=%async_computation.18 | async-start | bytes 4194304
  1045.4 15.5 %all-to-all-start.1 = ((bf16[8,192,96]{2,1,0:T(8,128)(2,1)}), bf16[8,192,96]{2,1,0:T(8,128)(2,1)S(1)}, u32[]{:S(2)}, u32[]{:S(2)}) async-start(bf16[8,192,96]{2,1,0:T(8,128)(2,1)} %bitcast.189), calls=%async_computation.5 | async-start | bytes 786432 | tf_op jit(solution)/shard_map/all_to_all | solution.py:20
  1053.8 12.5 %copy-start.60 = (f32[24]{0:T(128)S(1)}, f32[24]{0:T(128)}, u32[]{:S(2)}) copy-start(f32[24]{0:T(128)} %param.38) | copy-start | bytes 292
  1053.8 12.8 %copy-start.57 = (f32[768]{0:T(1024)S(1)}, f32[768]{0:T(1024)}, u32[]{:S(2)}) copy-start(f32[768]{0:T(1024)} %get-tuple-element.242) | copy-start | bytes 9220
  1061.7 62.3 %all-to-all-start = ((bf16[8,96,576]{2,1,0:T(8,128)(2,1)}), bf16[8,96,576]{2,1,0:T(8,128)(2,1)}, u32[]{:S(2)}, u32[]{:S(2)}) async-start(bf16[8,96,576]{2,1,0:T(8,128)(2,1)} %bitcast.22), calls=%async_computation.4 | async-start | bytes 1966080 | tf_op jit(solution)/shard_map/all_to_all | solution.py:20
  1066.3 54.6 %copy-start.2 = (f32[1024,768]{1,0:T(8,128)S(1)}, f32[1024,768]{1,0:T(8,128)}, u32[]{:S(2)}) copy-start(f32[1024,768]{1,0:T(8,128)} %copy-done.1) | copy-start | bytes 9437188
  1066.3 54.6 %copy-start.36 = (f32[1024]{0:T(1024)S(1)}, f32[1024]{0:T(1024)}, u32[]{:S(2)}) copy-start(f32[1024]{0:T(1024)} %copy-done.35) | copy-start | bytes 12292
  1066.3 54.6 %copy-start.39 = (f32[1024]{0:T(1024)S(1)}, f32[1024]{0:T(1024)}, u32[]{:S(2)}) copy-start(f32[1024]{0:T(1024)} %copy-done.38) | copy-start | bytes 12292
  1066.3 54.6 %copy-start.41 = (f32[1024]{0:T(1024)S(1)}, f32[1024]{0:T(1024)}, u32[]{:S(2)}) copy-start(f32[1024]{0:T(1024)} %copy-done.40) | copy-start | bytes 12292
  1066.3 54.6 %copy-start.48 = (f32[768]{0:T(1024)S(1)}, f32[768]{0:T(1024)}, u32[]{:S(2)}) copy-start(f32[768]{0:T(1024)} %get-tuple-element.239) | copy-start | bytes 9220
  (51 other events, 214.1 us)
Sparse Core Ops, SparseCore 0:
  10.4 50.5 all-gather.6
  275.4 58.9 reduce-scatter.4
  509.2 46.3 all-gather.14
  654.0 46.3 all-gather.16
Sparse Core Ops, SparseCore 1:
  278.0 41.5 all-gather.10
  339.6 46.2 all-gather.8
  387.9 41.3 all-gather.12
  438.6 57.1 reduce-scatter.6
  584.5 58.7 reduce-scatter.8
  967.5 58.7 reduce-scatter.10
where the time goes:
time: 1150 us; the launch traced here: 1140 us
  matrix products  402 us (35%)
  waiting for transfers between devices  358 us (31%)
  blocking collectives  214 us (19%)
  local copies, waits for them, and re-layouts  68.9 us (6%)
  other arithmetic  59.7 us (5%)
  starting transfers between devices  18.3 us (2%)
  between operations  16.6 us (1%)
    unnamed x2, blocking collectives  85.1 us
    dot_general x4, matrix products, attend_backward(): jnp.einsum('hqk,qhd->khd', grad_scores, query_seq, preferred_element_type...  79.2 us
    dot_general x4, matrix products, attend_backward(): jnp.einsum('hqk,khd->qhd', grad_scores, key_seq, preferred_element_type=j...  77.8 us
    dot_general x6, matrix products, matmul(): return jnp.dot(left_side, right_side, preferred_element_type=jnp.float32)  63.5 us
    reduce_scatter x1, waiting for transfers between devices, shards(): lax.psum_scatter(contract_cols(grad_pre, up_weight).astype(jnp.bfloat16),...  58.8 us
    dot_general x6, matrix products, contract_cols(): lax.dot_general(left_side, right_side, (((1,), (1,)), ((), ())), preferre...  58.7 us
    reduce_scatter x1, waiting for transfers between devices, shards(): lax.psum_scatter(matmul(mixed_rows, out_weight).astype(jnp.bfloat16), 'te...  58.1 us
    reduce_scatter x1, waiting for transfers between devices, shards(): lax.psum_scatter(matmul(act_low, down_weight).astype(jnp.bfloat16), 'tens...  56.9 us
  transfers between devices with their start and end apart: 14, of which 10 were waited for; matrix products, arithmetic and copies ran while one was open for 10% of the time, Pallas kernels for 0%

commit v1 on v0

v1 whole, which is shorter than its diff:
```python
import functools

import jax
import jax.numpy as jnp
from jax import lax
from jax.experimental import pallas as pl
from jax.experimental.pallas import tpu as pltpu
from jax.sharding import PartitionSpec as P

HEAD = 64
EPSILON = 1e-12
FLOOR_SCORE = -1e30
BLOCK = 256
WIDE = 256
BF16 = jnp.bfloat16
F32 = jnp.float32
VMEM_LIMIT = 60 * 1024 * 1024


def dot_nn(a, b):
    return lax.dot_general(a, b, (((1,), (0,)), ((), ())), preferred_element_type=F32)


def dot_nt(a, b):
    return lax.dot_general(a, b, (((1,), (1,)), ((), ())), preferred_element_type=F32)


def dot_tn(a, b):
    return lax.dot_general(a, b, (((0,), (0,)), ((), ())), preferred_element_type=F32)


def lane_iota(rows, lanes):
    return lax.broadcasted_iota(jnp.int32, (rows, lanes), 1)


def row_iota(rows, lanes):
    return lax.broadcasted_iota(jnp.int32, (rows, lanes), 0)


def head_mask(rows, h, extra):
    lane = lane_iota(rows, WIDE)
    keep = (lane >= h * HEAD) & (lane < (h + 1) * HEAD)
    if extra is not None:
        keep = keep | (lane >= extra)
    return keep


def normalize(v):
    center = v - jnp.mean(v, axis=-1, keepdims=True)
    inv = lax.rsqrt(jnp.mean(center * center, axis=-1, keepdims=True) + EPSILON)
    return center * inv, inv


def norm_back(g, n, inv):
    return inv * (
        g - jnp.mean(g, axis=-1, keepdims=True) - n * jnp.mean(g * n, axis=-1, keepdims=True)
    )


def split_three(v):
    hi = v.astype(BF16)
    rest = v - hi.astype(F32)
    mid = rest.astype(BF16)
    low = (rest - mid.astype(F32)).astype(BF16)
    return hi.astype(F32), mid.astype(F32), low.astype(F32)


def attend_kernel(len_ref, x_ref, w_ref, b_ref, ob_ref, res_ref, q_ref, k_ref, v_ref, mix_ref, lse_ref):
    t = pl.program_id(0)
    rows, width = x_ref.shape
    cols = mix_ref.shape[2]
    heads = cols // HEAD
    length = len_ref[0]
    lane = lane_iota(BLOCK, WIDE)

    @pl.when(t == 0)
    def _():
        @pl.loop(0, rows, step=BLOCK)
        def _(r):
            r = pl.multiple_of(r, BLOCK)
            res_ref[pl.ds(r, BLOCK), :] = x_ref[pl.ds(r, BLOCK), :].astype(F32) + ob_ref[...]

    @pl.loop(0, rows, step=BLOCK)
    def _(r):
        r = pl.multiple_of(r, BLOCK)
        here = pl.ds(r, BLOCK)
        out = dot_nn(x_ref[here, :], w_ref[0, :, : 3 * cols]) + b_ref[0]
        one = jnp.ones((BLOCK, WIDE - cols), F32)
        tail = lane_iota(BLOCK, WIDE - cols)
        position = r + row_iota(BLOCK, WIDE - cols)
        q_ref[0, here, :cols] = (out[:, :cols].astype(BF16).astype(F32) * HEAD**-0.5).astype(BF16)
        q_ref[0, here, cols:] = jnp.where(tail == 3, one, 0.0).astype(BF16)
        k_ref[0, here, :cols] = out[:, cols : 2 * cols].astype(BF16)
        bias = jnp.where(position < length, 0.0, FLOOR_SCORE)
        k_ref[0, here, cols:] = jnp.where(
            tail < 3, one, jnp.where(tail == 3, bias, 0.0)
        ).astype(BF16)
        v_ref[0, here, :cols] = out[:, 2 * cols : 3 * cols].astype(BF16)
        v_ref[0, here, cols:] = one.astype(BF16)

    @pl.loop(0, rows, step=BLOCK)
    def _(r):
        r = pl.multiple_of(r, BLOCK)
        here = pl.ds(r, BLOCK)
        query = q_ref[0, here, :]
        scores = [
            dot_nt(jnp.where(head_mask(BLOCK, h, cols), query, 0), k_ref[0]) for h in range(heads)
        ]
        mixed = jnp.zeros((BLOCK, WIDE), F32)
        total = jnp.zeros((BLOCK, 128), F32)
        for h in range(heads):
            top = jnp.max(scores[h], axis=-1, keepdims=True)
            terms = jnp.exp(scores[h] - top).astype(BF16)
            got = dot_nn(terms, v_ref[0])
            denom = got[:, cols : cols + 1]
            mixed = jnp.where(head_mask(BLOCK, h, None), got * (1.0 / denom), mixed)
            total = jnp.where(lane_iota(BLOCK, 128) == h, -(top + jnp.log(denom)), total)
        low = mixed[:, :cols].astype(BF16)
        mix_ref[0, here, :] = low
        lse_ref[0, here, :] = total
        res_ref[here, :] += dot_nt(low, w_ref[0, :, 3 * cols :])


def ffn_kernel(
    len_ref, res_ref, cot_ref, vec_ref, ub_ref, wu_ref, wd_ref,
    out_ref, gfirst_ref, gattn_ref, small_ref, gup_ref, gdn_ref,
    hid, hlow, acc, gb, act, dact, gpre,
):
    phase, t = pl.program_id(0), pl.program_id(1)
    last = pl.num_programs(1) - 1
    rows, width = res_ref.shape
    length = len_ref[0]
    gain_one, shift_one, down_bias = vec_ref[0:1, :], vec_ref[1:2, :], vec_ref[2:3, :]
    gain_two, shift_two = vec_ref[3:4, :], vec_ref[4:5, :]

    def blocks(body):
        @pl.loop(0, rows, step=BLOCK)
        def _(r):
            r = pl.multiple_of(r, BLOCK)
            body(r, pl.ds(r, BLOCK))

    def put(row, value):
        small_ref[row : row + 1, :] += jnp.sum(value, axis=0, keepdims=True)

    @pl.when((phase == 0) & (t == 0))
    def _():
        small_ref[...] = jnp.zeros_like(small_ref)

        def first(r, here):
            n, _ = normalize(res_ref[here, :])
            hidden = n * gain_one + shift_one
            hid[here, :] = hidden
            hlow[here, :] = hidden.astype(BF16)
            acc[here, :] = hidden + down_bias

        blocks(first)

    @pl.when(phase == 0)
    def _():
        def forward(r, here):
            pre = dot_nn(hlow[here, :], wu_ref[0]) + ub_ref[0]
            phi = 0.5 * (1.0 + lax.erf(pre * (0.5**0.5)))
            low = (pre * phi).astype(BF16)
            act[t, here, :] = low
            dact[t, here, :] = phi + pre * (jnp.exp(-0.5 * pre * pre) * 0.3989422804014327)
            acc[here, :] += dot_nt(low, wd_ref[0])

        blocks(forward)

    @pl.when((phase == 0) & (t == last))
    def _():
        def turn(r, here):
            n, inv = normalize(acc[here, :])
            valid = ((r + row_iota(BLOCK, 1)) < length).astype(F32)
            out_ref[here, :] = (n * gain_two + shift_two) * valid
            cot = cot_ref[here, :].astype(F32) * valid
            put(4, cot * n)
            put(5, cot)
            grad = norm_back(cot * gain_two, n, inv)
            acc[here, :] = grad
            low = grad.astype(BF16)
            gb[here, :] = low
            put(3, low.astype(F32))

        blocks(turn)

    @pl.when(phase == 1)
    def _():
        def backward(r, here):
            grad_act = dot_nn(gb[here, :], wd_ref[0]).astype(BF16).astype(F32)
            low = (grad_act * dact[t, here, :]).astype(BF16)
            gpre[here, :] = low
            part = dot_nt(low, wu_ref[0])

            @pl.when(t == 0)
            def _():
                hid[here, :] = part

            @pl.when(t > 0)
            def _():
                hid[here, :] += part

            small_ref[pl.ds(8 + t, 1), :] += jnp.sum(low.astype(F32), axis=0, keepdims=True)

        blocks(backward)

        @pl.loop(0, width, step=BLOCK)
        def _(c):
            c = pl.multiple_of(c, BLOCK)
            here = pl.ds(c, BLOCK)
            gdn_ref[0, here, :] = dot_tn(gb[:, here], act[t]).astype(BF16)
            gup_ref[0, here, :] = dot_tn(hlow[:, here], gpre[...]).astype(BF16)

    @pl.when((phase == 1) & (t == last))
    def _():
        def finish(r, here):
            grad_hidden = acc[here, :] + hid[here, :].astype(BF16).astype(F32)
            n, inv = normalize(res_ref[here, :])
            put(1, grad_hidden * n)
            put(2, grad_hidden)
            grad = norm_back(grad_hidden * gain_one, n, inv)
            gfirst_ref[here, :] = grad
            low = grad.astype(BF16)
            gattn_ref[here, :] = low
            put(0, low.astype(F32))

        blocks(finish)


def attend_back_kernel(
    x_ref, w_ref, gattn_ref, gfirst_ref, q_ref, k_ref, v_ref, mix_ref, lse_ref,
    gtok_ref, grad_ref, bias_ref,
    qh, gh, dq, kh, ds, dqkv,
):
    t = pl.program_id(0)
    rows, width = x_ref.shape
    cols = mix_ref.shape[2]
    heads = cols // HEAD

    @pl.when(t == 0)
    def _():
        gtok_ref[...] = gfirst_ref[...]

    bias_ref[...] = jnp.zeros_like(bias_ref)

    @pl.loop(0, rows, step=BLOCK)
    def _(r):
        r = pl.multiple_of(r, BLOCK)
        here = pl.ds(r, BLOCK)
        grad_mixed = dot_nn(gattn_ref[here, :], w_ref[0, :, 3 * cols :]).astype(BF16)
        product = grad_mixed.astype(F32) * mix_ref[0, here, :].astype(F32)
        lane = lane_iota(BLOCK, WIDE)
        wide = jnp.concatenate(
            [grad_mixed.astype(F32), jnp.zeros((BLOCK, WIDE - cols), F32)], axis=1
        )
        query = q_ref[0, here, :].astype(F32)
        key = k_ref[0, here, :]
        for h in range(heads):
            inside = (lane_iota(BLOCK, cols) >= h * HEAD) & (lane_iota(BLOCK, cols) < (h + 1) * HEAD)
            delta = jnp.sum(jnp.where(inside, product, 0.0), axis=-1, keepdims=True)
            hi, mid, low = split_three(-delta)
            keep = head_mask(BLOCK, h, None)
            tail = jnp.where(lane == cols, hi, jnp.where(lane == cols + 1, mid, jnp.where(lane == cols + 2, low, 0.0)))
            gh[h, here, :] = jnp.where(keep, wide, tail).astype(BF16)
            hi, mid, low = split_three(lse_ref[0, here, h : h + 1])
            tail = jnp.where(lane == cols, hi, jnp.where(lane == cols + 1, mid, jnp.where(lane == cols + 2, low, 0.0)))
            tail = jnp.where(lane == cols + 3, 1.0, tail)
            qh[h, here, :] = jnp.where(keep, query, tail).astype(BF16)
            kh[h, here, :] = jnp.where(keep, key, 0)

    @pl.loop(0, rows, step=BLOCK)
    def _(r):
        r = pl.multiple_of(r, BLOCK)
        here = pl.ds(r, BLOCK)
        key, value = k_ref[0, here, :], v_ref[0, here, :]
        grad_key = jnp.zeros((BLOCK, WIDE), F32)
        grad_value = jnp.zeros((BLOCK, WIDE), F32)
        logits = [dot_nt(key, qh[h]) for h in range(heads)]
        grads = [dot_nt(value, gh[h]) for h in range(heads)]
        for h in range(heads):
            prob = jnp.exp(logits[h])
            grad_value += dot_nn(prob.astype(BF16), gh[h])
            grad_score = (prob * grads[h]).astype(BF16)
            grad_key += dot_nn(grad_score, qh[h])
            part = dot_tn(grad_score, kh[h, here, :])
            if h == 0:
                total = part
            else:
                total += part

        @pl.when(r == 0)
        def _():
            dq[...] = total

        @pl.when(r > 0)
        def _():
            dq[...] += total

        low = grad_key[:, :cols].astype(BF16)
        dqkv[here, cols : 2 * cols] = low
        low = grad_value[:, :cols].astype(BF16)
        dqkv[here, 2 * cols :] = low
        bias_ref[0, 1:2, :] += jnp.sum(low.astype(F32), axis=0, keepdims=True)

    @pl.loop(0, rows, step=BLOCK)
    def _(r):
        r = pl.multiple_of(r, BLOCK)
        here = pl.ds(r, BLOCK)
        low = (dq[here, :cols] * HEAD**-0.5).astype(BF16)
        dqkv[here, :cols] = low
        bias_ref[0, 0:1, :] += jnp.sum(low.astype(F32), axis=0, keepdims=True)
        gtok_ref[here, :] += dot_nt(dqkv[here, :], w_ref[0, :, : 3 * cols])

    @pl.loop(0, width, step=BLOCK)
    def _(c):
        c = pl.multiple_of(c, BLOCK)
        here = pl.ds(c, BLOCK)
        grad_ref[0, here, : 3 * cols] = dot_tn(x_ref[:, here], dqkv[...]).astype(BF16)
        grad_ref[0, here, 3 * cols :] = dot_tn(gattn_ref[:, here], mix_ref[0]).astype(BF16)


def resident(shape):
    return pl.BlockSpec(shape, lambda *ids: (0,) * len(shape), pipeline_mode=pl.Buffered(1))


def result(shape):
    return pl.BlockSpec(shape, lambda *ids: (0,) * len(shape))


def per_step(shape):
    return pl.BlockSpec((1, *shape[1:]), lambda t: (t, 0, 0))


def struct(shape, dtype):
    return jax.ShapeDtypeStruct(shape, dtype)


def params(steps):
    return pltpu.CompilerParams(
        dimension_semantics=("arbitrary",) * steps, vmem_limit_bytes=VMEM_LIMIT
    )


def run_attend(length, tokens, w_attn, bias, out_bias):
    rows, width = tokens.shape
    groups = w_attn.shape[0]
    cols = width // groups
    wide = (groups, rows, WIDE)
    return pl.pallas_call(
        attend_kernel,
        grid=(groups,),
        in_specs=[
            pl.BlockSpec(memory_space=pltpu.SMEM),
            resident((rows, width)),
            per_step(w_attn.shape),
            per_step(bias.shape),
            resident(out_bias.shape),
        ],
        out_specs=[
            result((rows, width)),
            per_step(wide), per_step(wide), per_step(wide),
            per_step((groups, rows, cols)), per_step((groups, rows, 128)),
        ],
        out_shape=[
            struct((rows, width), F32),
            struct(wide, BF16), struct(wide, BF16), struct(wide, BF16),
            struct((groups, rows, cols), BF16), struct((groups, rows, 128), F32),
        ],
        compiler_params=params(1),
        name="attend",
    )(length, tokens, w_attn, bias, out_bias)


def run_ffn(length, residual, cotangent, vectors, up_bias, w_up, w_down):
    rows, width = residual.shape
    groups = w_up.shape[0]
    units = w_up.shape[2]
    slab = pl.BlockSpec((1, width, units), lambda p, t: (t, 0, 0))
    grad = pl.BlockSpec((1, width, units), lambda p, t: (p * t, 0, 0))
    return pl.pallas_call(
        ffn_kernel,
        grid=(2, groups),
        in_specs=[
            pl.BlockSpec(memory_space=pltpu.SMEM),
            resident((rows, width)),
            resident((rows, width)),
            resident(vectors.shape),
            pl.BlockSpec((1, 1, units), lambda p, t: (t, 0, 0)),
            slab, slab,
        ],
        out_specs=[
            result((rows, width)), result((rows, width)), result((rows, width)), result((16, width)),
            grad, grad,
        ],
        out_shape=[
            struct((rows, width), F32), struct((rows, width), F32), struct((rows, width), BF16),
            struct((16, width), F32),
            struct(w_up.shape, BF16), struct(w_up.shape, BF16),
        ],
        scratch_shapes=[
            pltpu.VMEM((rows, width), F32), pltpu.VMEM((rows, width), BF16),
            pltpu.VMEM((rows, width), F32), pltpu.VMEM((rows, width), BF16),
            pltpu.VMEM((groups, rows, units), BF16), pltpu.VMEM((groups, rows, units), F32),
            pltpu.VMEM((rows, units), BF16),
        ],
        compiler_params=params(2),
        name="ffn",
    )(length, residual, cotangent, vectors, up_bias, w_up, w_down)


def run_attend_back(tokens, w_attn, grad_attn, grad_first, q, k, v, mixed, lse):
    rows, width = tokens.shape
    groups = w_attn.shape[0]
    cols = width // groups
    heads = cols // HEAD
    return pl.pallas_call(
        attend_back_kernel,
        grid=(groups,),
        in_specs=[
            resident((rows, width)), per_step(w_attn.shape),
            resident((rows, width)), resident((rows, width)),
            per_step(q.shape), per_step(k.shape), per_step(v.shape),
            per_step(mixed.shape), per_step(lse.shape),
        ],
        out_specs=[result((rows, width)), per_step(w_attn.shape), per_step((groups, 8, cols))],
        out_shape=[
            struct((rows, width), F32), struct(w_attn.shape, BF16), struct((groups, 8, cols), F32),
        ],
        scratch_shapes=[
            pltpu.VMEM((heads, rows, WIDE), BF16), pltpu.VMEM((heads, rows, WIDE), BF16),
            pltpu.VMEM((rows, WIDE), F32), pltpu.VMEM((heads, rows, WIDE), BF16),
            pltpu.VMEM((8, 128), BF16), pltpu.VMEM((rows, 3 * cols), BF16),
        ],
        compiler_params=params(1),
        name="attend_back",
    )(tokens, w_attn, grad_attn, grad_first, q, k, v, mixed, lse)


def shards(
    tokens, lengths, w_query, w_key, w_value, w_out, w_up, w_down,
    query_bias, value_bias, out_bias, attn_gain, attn_shift, up_bias, down_bias, ffn_gain, ffn_shift,
    cotangent,
):
    rows, width = tokens.shape
    groups = lax.axis_size("tensor")
    spans = lax.axis_size("dp")
    seq_count = lengths.shape[0]
    assert rows * groups == seq_count * rows and seq_count == groups
    rank = lax.axis_index("tensor")
    length = lax.dynamic_slice_in_dim(lengths, rank, 1)
    both = ("dp", "tensor")

    pack = jnp.concatenate([w_query, w_key, w_value, w_out.T, w_up, w_down.T], axis=1)
    whole = lax.all_gather(pack, both, axis=0, tiled=True)
    whole = whole.reshape(spans, groups, *pack.shape).swapaxes(0, 1)
    whole = whole.reshape(groups, width, pack.shape[1])
    cols = width // groups
    units = w_up.shape[1]
    w_attn, w_in, w_back = whole[:, :, : 4 * cols], whole[:, :, 4 * cols : 4 * cols + units], whole[:, :, 4 * cols + units :]

    vectors = (query_bias, value_bias, out_bias, attn_gain, attn_shift, down_bias, ffn_gain, ffn_shift)
    count = query_bias.shape[0]
    flat = jnp.concatenate([jnp.stack(vectors).reshape(-1), up_bias])
    gathered = lax.all_gather(flat, both, axis=0, tiled=True).reshape(spans * groups, -1)
    full = gathered[:, : 8 * count].reshape(-1, 8, count).swapaxes(0, 1).reshape(8, width)
    ub = gathered[:, 8 * count :].reshape(groups, 1, units)
    qb, vb = full[0].reshape(groups, 1, cols), full[1].reshape(groups, 1, cols)
    bias = jnp.concatenate([qb, jnp.zeros_like(qb), vb], axis=2)

    residual, q, k, v, mixed, lse = run_attend(length, tokens, w_attn, bias, full[2:3])
    output, grad_first, grad_attn, small, grad_in, grad_back = run_ffn(
        length, residual, cotangent, full[3:8], ub, w_in, w_back
    )
    grad_tokens, grad_attn_w, bias_grad = run_attend_back(
        tokens, w_attn, grad_attn, grad_first, q, k, v, mixed, lse
    )

    every = jnp.concatenate([grad_attn_w, grad_in, grad_back], axis=2)
    every = every.reshape(groups, spans, width // spans, -1).swapaxes(0, 1)
    every = every.reshape(spans * groups * (width // spans), -1)
    owned = lax.psum_scatter(every, both, scatter_dimension=0, tiled=True).astype(F32)

    rows8 = jnp.concatenate(
        [bias_grad[:, 0].reshape(1, width), bias_grad[:, 1].reshape(1, width), small[:6]]
    )
    parts = jnp.concatenate(
        [
            rows8.reshape(8, spans * groups, count).swapaxes(0, 1).reshape(spans * groups, 8 * count),
            small[8 : 8 + groups].reshape(spans * groups, -1),
        ],
        axis=1,
    )
    tiny = lax.psum_scatter(parts.reshape(-1), both, scatter_dimension=0, tiled=True)
    tiny8 = tiny[: 8 * count].reshape(8, count)
    return (
        output, grad_tokens,
        owned[:, :cols], owned[:, cols : 2 * cols], owned[:, 2 * cols : 3 * cols],
        owned[:, 3 * cols : 4 * cols].T,
        owned[:, 4 * cols : 4 * cols + units], owned[:, 4 * cols + units :].T,
        tiny8[0], tiny8[1], tiny8[2], tiny8[3], tiny8[4], tiny[8 * count :], tiny8[5], tiny8[6], tiny8[7],
    )


def solution(mesh):
    rows, vector, matrix, flipped = (
        P(("dp", "tensor"), None), P(("dp", "tensor")), P("dp", "tensor"), P("tensor", "dp"),
    )
    return jax.shard_map(
        shards,
        mesh=mesh,
        in_specs=(rows, P("dp"), matrix, matrix, matrix, flipped, matrix, flipped, *(vector,) * 9, rows),
        out_specs=(rows, rows, matrix, matrix, matrix, flipped, matrix, flipped, *(vector,) * 9),
        check_vma=False,
    )
```

time: 1150 us -> 494 us (0.43)
  matrix products: 402 us -> 0 us
  waiting for transfers between devices: 358 us -> 176 us
  Pallas kernels: 0 us -> 177 us
  blocking collectives: 214 us -> 82.1 us
  other arithmetic: 59.7 us -> 9.68 us
  local copies, waits for them, and re-layouts: 68.9 us -> 34.1 us
  starting transfers between devices: 18.3 us -> 0.08 us
    dot_general x46 -> x0, matrix products: 402 us -> none  [the longest x4 79.2 us: attend_backward(): jnp.einsum('hqk,qhd->khd', grad_scores, query_seq, preferred_element_type...]
    pallas_call x0 -> x3, Pallas kernels: none -> 177 us  [the longest x1 76.7 us: run_attend_back(): pl.pallas_call(attend_back_kernel, grid=(groups,), in_specs=[resident((ro...]
    all_gather x4 -> x0, blocking collectives: 129 us -> none  [the longest x1 33.3 us: shards(): lax.all_gather(w_key, 'dp', axis=0, tiled=True)]
    all_gather x6 -> x1, waiting for transfers between devices: 146 us -> 57.9 us  [shards(): whole = lax.all_gather(pack, both, axis=0, tiled=True)]
    reduce_scatter x4 -> x1, waiting for transfers between devices: 174 us -> 118 us  [shards(): lax.psum_scatter(every, both, scatter_dimension=0, tiled=True).astype(F32)]
    reduce_sum x20 -> x0, other arithmetic: 43.1 us -> none  [the longest x4 12.7 us: attend_forward(): row_total = jnp.sum(exp_terms, axis=-1, keepdims=True)]
    all_to_all x4 -> x0, waiting for transfers between devices: 36.1 us -> none  [sum_at_owner(): lax.all_to_all(parts, axis, split_axis=0, concat_axis=0, tiled=True)]
    unnamed x157 -> x6, local copies, waits for them, and re-layouts: 25.3 us -> 2.49 us
  transfers between devices with their start and end apart: 14 -> 2, of which waited for: 10 -> 2; matrix products, arithmetic and copies ran while one was open for 10% -> 2% of each run, Pallas kernels for 0% -> 0%
where the time goes in v1:
time: 494 us; the launch traced here: 493 us
  Pallas kernels  177 us (36%)
  waiting for transfers between devices  176 us (36%)
  blocking collectives  82.1 us (17%)
  local copies, waits for them, and re-layouts  34.1 us (7%)
  between operations  14.2 us (3%)
  other arithmetic  9.68 us (2%)
    reduce_scatter x1, waiting for transfers between devices, shards(): lax.psum_scatter(every, both, scatter_dimension=0, tiled=True).astype(F32)  118 us
    unnamed x2, blocking collectives  82.1 us
    pallas_call x1, Pallas kernels, run_attend_back(): pl.pallas_call(attend_back_kernel, grid=(groups,), in_specs=[resident((ro...  76.7 us
    pallas_call x1, Pallas kernels, run_ffn(): pl.pallas_call(ffn_kernel, grid=(2, groups), in_specs=[pl.BlockSpec(memor...  60.9 us
    all_gather x1, waiting for transfers between devices, shards(): whole = lax.all_gather(pack, both, axis=0, tiled=True)  57.9 us
    pallas_call x1, Pallas kernels, run_attend(): pl.pallas_call(attend_kernel, grid=(groups,), in_specs=[pl.BlockSpec(memo...  39 us
  transfers between devices with their start and end apart: 2, of which 2 were waited for; matrix products, arithmetic and copies ran while one was open for 2% of the time, Pallas kernels for 0%

profile of v1, /device:TPU:0, one launch (start us, length us, event | category | flops | bytes accessed | tf_op | source)
XLA Modules:
  0.0 493.1 jit_solution(455332371361573159)
XLA Ops:
  7.2 0.9 copy.48
  8.1 1.9 concatenate.25
  10.2 0.8 stack.35
  11.0 0.8 maximum_dynamic-update-slice_fusion
  11.9 43.1 %all-reduce = f32[9216]{0:T(1024)S(1)} all-reduce(f32[9216]{0:T(1024)S(1)} %maximum_dynamic-update-slice_fusion), channel_id=1, replica_groups=mesh['dp'=8,'tensor'=4] {'dp','tensor'}, use_global_device_ids=true, to_apply=%add | all-reduce | flops 9216 | bytes 73728
  55.3 0.1 slice_reduce_fusion
  55.6 0.7 slice.114.ob_ref
  56.3 0.7 slice.116.vec_ref
  57.0 0.7 reshape.102.ub_ref
  57.8 1.2 dynamic_slice.3.len_ref
  59.0 0.6 pad_maximum_fusion.2.b_ref
  59.6 57.9 %all-gather.2.cloned.1.call-done = bf16[3072,2304]{1,0:T(8,128)(2,1)} async-done(((bf16[96,2304]{1,0:T(8,128)(2,1)}), bf16[3072,2304]{1,0:T(8,128)(2,1)}) %all-gather.2.cloned.1.call-update) | async-done | bytes 14155792 | tf_op jit(solution)/shard_map/all_gather | solution.py:454
  117.5 6.8 %copy.49 = bf16[8,4,96,2304]{3,2,0,1:T(8,128)(2,1)S(1)} copy(bf16[8,4,96,2304]{3,2,1,0:T(8,128)(2,1)} %bitcast.28) | data formatting | bytes 28311552 | tf_op jit(solution)/shard_map/reshape | solution.py:455
  124.3 5.5 %fusion = (bf16[4,768,768]{2,1,0:T(8,128)(2,1)}, bf16[4,768,768]{2,1,0:T(8,128)(2,1)}, bf16[4,768,768]{2,1,0:T(8,128)(2,1)}) fusion(bf16[4,768,2304]{2,1,0:T(8,128)(2,1)S(1)} %bitcast.26), kind=kLoop, calls=%fused_computation.12 | loop fusion | bytes 28311552 | tf_op jit(solution)/shard_map/slice | solution.py:459
  129.8 39.0 %attend.1 = (f32[1024,768]{1,0:T(8,128)}, bf16[4,1024,256]{2,1,0:T(8,128)(2,1)}, bf16[4,1024,256]{2,1,0:T(8,128)(2,1)}, bf16[4,1024,256]{2,1,0:T(8,128)(2,1)}, b...) custom-call(s32[1]{0:T(128)} %dynamic_slice.3.len_ref, bf16[1024,768]{1,0:T(8,128)(2,1)} %x_ref.3, ...), custom_call_target="tpu_custom_call" | custom-call | tf_op jit(solution)/shard_map/attend/pallas_call | solution.py:349
  168.9 60.9 %ffn.1 = (f32[1024,768]{1,0:T(8,128)}, f32[1024,768]{1,0:T(8,128)}, bf16[1024,768]{1,0:T(8,128)(2,1)}, f32[16,768]{1,0:T(8,128)}, bf16[4,768,768]{2,1,0:T(8,128)(2,1)}, /*index=5*/bf16[4,768,768]{2,1,0:T(8,128)(2,1)}) custom-call(s32[1]{0:T(128)} %dynamic_slice.3.len_ref, f32[1024,768]{1,0:T(8,128)} %get-tuple-element.32.res_ref, bf16[1024,768]{1,0:T(8,128)(2,1)} %cot_ref.1, ...), custom_call_target="tpu_custom_call" | custom-call | tf_op jit(solution)/shard_map/ffn/pallas_call | solution.py:380
  229.7 76.7 %attend_back.1 = (f32[1024,768]{1,0:T(8,128)}, bf16[4,768,768]{2,1,0:T(8,128)(2,1)}, f32[4,8,192]{2,1,0:T(8,128)}) custom-call(bf16[1024,768]{1,0:T(8,128)(2,1)} %x_ref.3, bf16[4,768,768]{2,1,0:T(8,128)(2,1)} %get-tuple-element.105.w_ref, bf16[1024,768]{1,0:T(8,128)(2,1)} %get-tuple-element.34.gattn_ref, f32[1024,768]{1,0:T(8,128)} %get-tuple-element.35.gfirst_ref, ...), custom_call_target="tpu_custom_call" | custom-call | tf_op jit(solution)/shard_map/attend_back/pallas_call | solution.py:416
  306.5 7.1 %pad_maximum_fusion = bf16[4,768,2304]{2,1,0:T(8,128)(2,1)S(1)} fusion(bf16[4,768,768]{2,1,0:T(8,128)(2,1)} %get-tuple-element.44, bf16[4,768,768]{2,1,0:T(8,128)(2,1)} %get-tuple-element.43, bf16[4,768,768]{2,1,0:T(8,128)(2,1)} %get-tuple-element.42), kind=kLoop, calls=%fused_computation | loop fusion | flops 42467328 | bytes 28311552 | tf_op jit(solution)/shard_map/concatenate | solution.py:478
  313.5 5.7 %copy.53 = bf16[8,4,96,2304]{3,2,1,0:T(8,128)(2,1)} copy(bf16[8,4,96,2304]{3,2,0,1:T(8,128)(2,1)S(1)} %bitcast.27) | data formatting | bytes 28311552 | tf_op jit(solution)/shard_map/transpose | solution.py:479
  319.2 0.8 copy-done
  320.0 0.9 slice_reduce_fusion.4
  321.0 0.1 concatenate.31
  321.2 0.1 reshape.105
  321.6 39.0 %all-reduce.1 = f32[9216]{0:T(1024)S(1)} all-reduce(f32[9216]{0:T(1024)S(1)} %reshape.107), channel_id=3, replica_groups=mesh['dp'=8,'tensor'=4] {'dp','tensor'}, use_global_device_ids=true, to_apply=%region_1.0.clone | all-reduce | flops 9216 | bytes 73728
  360.7 0.6 slice.135
  361.3 0.6 fusion.2
  361.9 118.5 %reduce-scatter.2.cloned.1.call-done = bf16[96,2304]{1,0:T(8,128)(2,1)} async-done(((bf16[3072,2304]{1,0:T(8,128)(2,1)}), bf16[96,2304]{1,0:T(8,128)(2,1)}) %reduce-scatter.2.cloned.1.call-update) | async-done | bytes 442384 | tf_op jit(solution)/shard_map/reduce_scatter | solution.py:481
  480.4 1.1 convert_element_type.3
  481.4 0.7 slice_bitcast_fusion
  482.3 0.7 copy.55
  483.0 1.6 fusion.1
  484.6 1.6 slice.152
  (28 shorter events, 1.4 us)
Async XLA Ops:
  7.2 110.3 %all-gather.2.cloned.1.call-start = ((), (), s32[]{:S(2)}) async-start(), calls=%async_computation.1 | async-start | bytes 14598144 | tf_op jit(solution)/shard_map/all_gather | solution.py:454
  10.1 470.3 %reduce-scatter.2.cloned.1.call-start = ((), (), s32[]{:S(2)}) async-start(), calls=%async_computation.2 | async-start | bytes 14598144 | tf_op jit(solution)/shard_map/reduce_scatter | solution.py:481
  319.2 0.8 copy-start
Sparse Core Ops, SparseCore 0:
  11.5 105.9 all-gather.1
  319.3 160.9 reduce-scatter.1

commit v2 on v1

--- a/solution.py
+++ b/solution.py
@@ -65,26 +65,173 @@
     return hi.astype(F32), mid.astype(F32), low.astype(F32)
 
 
-def attend_kernel(len_ref, x_ref, w_ref, b_ref, ob_ref, res_ref, q_ref, k_ref, v_ref, mix_ref, lse_ref):
-    t = pl.program_id(0)
+MESH = pl.DeviceIdType.MESH
+DEPTH = 4
+SLOTS = 11
+
+
+def around(z, k):
+    return lax.rem(z + k, DEPTH)
+
+
+class Place:
+    def __init__(self):
+        dp, t = lax.axis_index("dp"), lax.axis_index("tensor")
+        self.z, self.x = lax.div(dp, 2), lax.rem(dp, 2)
+        self.y, self.c = lax.div(t, 2), lax.rem(t, 2)
+
+    def device(self, z=None, x=None, y=None, c=None):
+        z, x = self.z if z is None else z, self.x if x is None else x
+        y, c = self.y if y is None else y, self.c if c is None else c
+        return (z * 2 + x, y * 2 + c)
+
+    def neighbours(self):
+        return [self.device(z=around(self.z, k)) for k in range(1, DEPTH)] + [
+            self.device(x=1 - self.x), self.device(y=1 - self.y), self.device(c=1 - self.c),
+        ]
+
+    def greet(self):
+        barrier = pltpu.get_barrier_semaphore()
+        peers = self.neighbours()
+        for peer in peers:
+            pl.semaphore_signal(barrier, inc=1, device_id=peer, device_id_type=MESH)
+        pl.semaphore_wait(barrier, len(peers))
+
+    def group(self, step):
+        y = lax.rem(self.y + lax.div(step, 2), 2)
+        c = lax.rem(self.c + lax.rem(step, 2), 2)
+        return y * 2 + c
+
+
+class Spread:
+    def __init__(self, place, own, buf, send, recv, home, first):
+        self.p, self.own, self.buf, self.send, self.recv, self.home = place, own, buf, send, recv, home
+        self.first = first
+        self.to_a = place.device(x=1 - place.x) if first == "x" else place.device(y=1 - place.y)
+        self.to_b = place.device(y=1 - place.y) if first == "x" else place.device(x=1 - place.x)
+        self.to_c = place.device(c=1 - place.c)
+
+    def at(self, z, a=0, b=0, c=0):
+        p = self.p
+        dx, dy = (a, b) if self.first == "x" else (b, a)
+        y = p.y if dy == 0 else 1 - p.y
+        x = p.x if dx == 0 else 1 - p.x
+        return self.buf.at[y, p.c if c == 0 else 1 - p.c, z, x]
+
+    def chip(self, dy, c=0):
+        p = self.p
+        return self.buf.at[p.y if dy == 0 else 1 - p.y, p.c if c == 0 else 1 - p.c]
+
+    def copy(self, src, dst, slot, device):
+        return pltpu.make_async_remote_copy(
+            src_ref=src, dst_ref=dst, send_sem=self.send.at[slot], recv_sem=self.recv.at[slot],
+            device_id=device, device_id_type=MESH,
+        )
+
+    def arrive(self, ref, slot, device):
+        self.copy(ref, ref, slot, device).wait_recv()
+
+    def local(self):
+        return pltpu.make_async_copy(self.own, self.at(self.p.z), self.home)
+
+    def begin(self):
+        p = self.p
+        self.local().start()
+        for k in range(1, DEPTH):
+            self.copy(self.own, self.at(p.z), k - 1, p.device(z=around(p.z, k))).start()
+        self.copy(self.own, self.at(p.z), 3, self.to_a).start()
+
+    def after_z(self):
+        p = self.p
+        for k in range(1, DEPTH):
+            ref = self.at(around(p.z, DEPTH - k))
+            self.arrive(ref, k - 1, p.device(z=around(p.z, k)))
+            self.copy(ref, ref, 3 + DEPTH - k, self.to_a).start()
+        self.local().wait()
+        ref = self.at(slice(None))
+        self.copy(ref, ref, 7, self.to_b).start()
+
+    def after_a(self):
+        for k in range(DEPTH):
+            self.arrive(self.at(around(self.p.z, k), a=1), 3 + k, self.to_a)
+        ref = self.at(slice(None), a=1)
+        self.copy(ref, ref, 8, self.to_b).start()
+        if self.first == "x":
+            self.swap(0)
+
+    def swap(self, dy):
+        ref = self.chip(dy)
+        self.copy(ref, ref, 9 + dy, self.to_c).start()
+
+    def after_b(self):
+        self.arrive(self.at(slice(None), b=1), 7, self.to_b)
+        if self.first == "y":
+            self.swap(0)
+        self.arrive(self.at(slice(None), a=1, b=1), 8, self.to_b)
+        self.swap(1)
+
+    def after_c(self, dy):
+        self.arrive(self.chip(dy, c=1), 9 + dy, self.to_c)
+
+    def finish(self):
+        p = self.p
+        one, column, chip = self.at(p.z), self.at(slice(None)), self.chip(0)
+        sizes = [(one, p.device(z=around(p.z, k))) for k in range(1, DEPTH)] + [(one, self.to_a)] * DEPTH
+        sizes += [(column, self.to_b)] * 2 + [(chip, self.to_c)] * 2
+        for slot, (ref, device) in enumerate(sizes):
+            self.copy(ref, ref, slot, device).wait_send()
+
+
+def segment_tables():
+    lane = jnp.arange(768, dtype=jnp.int32)
+    rows = jnp.stack([lane % 24, lane // 24, lane % 96, lane // 96])
+    return jnp.concatenate([rows, jnp.zeros_like(rows)])
+
+
+def one_hot(tab_ref, row, start, rows):
+    return (row_iota(rows, tab_ref.shape[1]) == start + tab_ref[row : row + 1, :]).astype(BF16)
+
+
+def join_vectors(block_ref, tab_ref, vec_ref):
+    pieces = jnp.sum(block_ref[...].reshape(32, 8, 384), axis=1)
+    parts = jnp.concatenate(split_three(pieces), axis=0).astype(BF16)
+    width = vec_ref.shape[1]
+    row = row_iota(32, width)
+    owner = lax.shift_left(row & 7, 2) + lax.shift_right_logical(row, 3)
+
+    def place(start, table):
+        got = dot_nn(parts, one_hot(tab_ref, table, start, 384))
+        return got[:32] + got[32:64] + got[64:]
+
+    for j in range(8):
+        keep = owner == tab_ref[1:2, :]
+        vec_ref[j : j + 1, :] = jnp.sum(jnp.where(keep, place(24 * j, 0), 0.0), axis=0, keepdims=True)
+    got = place(192, 2)
+    for k in range(4):
+        keep = owner == tab_ref[3:4, :] + 8 * k
+        vec_ref[8 + k : 9 + k, :] = jnp.sum(jnp.where(keep, got, 0.0), axis=0, keepdims=True)
+    vec_ref[12:, :] = jnp.zeros((vec_ref.shape[0] - 12, width), F32)
+
+
+def attend_steps(
+    length, hook, x_ref, w_ref, bias_ref, g, out_bias, res_ref, q_ref, k_ref, v_ref, mix_ref, lse_ref, first
+):
     rows, width = x_ref.shape
     cols = mix_ref.shape[2]
     heads = cols // HEAD
-    length = len_ref[0]
-    lane = lane_iota(BLOCK, WIDE)
-
-    @pl.when(t == 0)
+
+    @pl.when(first)
     def _():
         @pl.loop(0, rows, step=BLOCK)
         def _(r):
             r = pl.multiple_of(r, BLOCK)
-            res_ref[pl.ds(r, BLOCK), :] = x_ref[pl.ds(r, BLOCK), :].astype(F32) + ob_ref[...]
+            res_ref[pl.ds(r, BLOCK), :] = x_ref[pl.ds(r, BLOCK), :].astype(F32) + out_bias[...]
 
     @pl.loop(0, rows, step=BLOCK)
     def _(r):
         r = pl.multiple_of(r, BLOCK)
         here = pl.ds(r, BLOCK)
-        out = dot_nn(x_ref[here, :], w_ref[0, :, : 3 * cols]) + b_ref[0]
+        out = dot_nn(x_ref[here, :], w_ref[0, :, : 3 * cols]) + bias_ref[g, 0:1, :]
         one = jnp.ones((BLOCK, WIDE - cols), F32)
         tail = lane_iota(BLOCK, WIDE - cols)
         position = r + row_iota(BLOCK, WIDE - cols)
@@ -101,6 +248,7 @@
     @pl.loop(0, rows, step=BLOCK)
     def _(r):
         r = pl.multiple_of(r, BLOCK)
+        hook(r)
         here = pl.ds(r, BLOCK)
         query = q_ref[0, here, :]
         scores = [
@@ -121,8 +269,94 @@
         res_ref[here, :] += dot_nt(low, w_ref[0, :, 3 * cols :])
 
 
+def attend_kernel(len_ref, x_ref, w_ref, bias_ref, ob_ref, *outs):
+    t = pl.program_id(0)
+    attend_steps(len_ref[0], lambda r: None, x_ref, w_ref, bias_ref, t, ob_ref, *outs, t == 0)
+
+
+def attend_spread_kernel(
+    len_ref, tab_ref, x_ref, own_vec, own_attn, own_up, own_down,
+    res_ref, q_ref, k_ref, v_ref, mix_ref, lse_ref, w_ref, vec_ref, up_ref, down_ref,
+    vec_buf, attn_buf, bias_buf, send, recv, home,
+):
+    t = pl.program_id(0)
+    place = Place()
+    cols = mix_ref.shape[2]
+
+    def spread(n, own, buf, first):
+        return Spread(place, own, buf, send.at[n], recv.at[n], home.at[n], first)
+
+    small = spread(0, own_vec, vec_buf, "x")
+    attn = spread(1, own_attn, attn_buf, "x")
+    up = spread(2, own_up, up_ref, "y")
+    down = spread(3, own_down, down_ref, "x")
+
+    @pl.when(t == 0)
+    def _():
+        place.greet()
+        small.begin()
+        attn.begin()
+        small.after_z()
+        small.after_a()
+        small.after_b()
+        small.after_c(0)
+        small.after_c(1)
+        join_vectors(vec_buf, tab_ref, vec_ref)
+        for g in range(bias_buf.shape[0]):
+            there = slice(g * cols, (g + 1) * cols)
+            bias_buf[g, 0:1, :] = jnp.concatenate(
+                [vec_ref[0:1, there], jnp.zeros((1, cols), F32), vec_ref[1:2, there]], axis=1
+            )
+        attn.after_z()
+        attn.after_a()
+        up.begin()
+        down.begin()
+
+    @pl.when(t == 1)
+    def _():
+        attn.after_c(0)
+
+    @pl.when(t == 3)
+    def _():
+        attn.after_c(1)
+
+    def hook(r):
+        def at(step, block, *events):
+            @pl.when((t == step) & (r == block * BLOCK))
+            def _():
+                for event in events:
+                    event()
+
+        at(0, 3, up.after_z)
+        at(1, 1, attn.after_b, down.after_z)
+        at(1, 3, up.after_a)
+        at(2, 2, down.after_a)
+        at(3, 1, up.after_b)
+
+    g = place.group(t)
+    y, c = lax.div(g, 2), lax.rem(g, 2)
+    for z in range(DEPTH):
+        for x in range(2):
+            n = attn_buf.shape[4]
+            start = (z * 2 + x) * n
+            w_ref[0, start : start + n, :] = attn_buf[y, c, z, x]
+    attend_steps(
+        len_ref[lax.axis_index("tensor")], hook, x_ref, w_ref, bias_buf, g, vec_ref.at[2:3],
+        res_ref, q_ref, k_ref, v_ref, mix_ref, lse_ref, t == 0,
+    )
+
+    @pl.when(t == pl.num_programs(0) - 1)
+    def _():
+        down.after_b()
+        for piece in (up, down):
+            piece.after_c(0)
+            piece.after_c(1)
+        for piece in (small, attn, up, down):
+            piece.finish()
+
+
 def ffn_kernel(
-    len_ref, res_ref, cot_ref, vec_ref, ub_ref, wu_ref, wd_ref,
+    len_ref, res_ref, cot_ref, vec_ref, wu_ref, wd_ref,
     out_ref, gfirst_ref, gattn_ref, small_ref, gup_ref, gdn_ref,
     hid, hlow, acc, gb, act, dact, gpre,
 ):
@@ -130,8 +364,8 @@
     last = pl.num_programs(1) - 1
     rows, width = res_ref.shape
     length = len_ref[0]
-    gain_one, shift_one, down_bias = vec_ref[0:1, :], vec_ref[1:2, :], vec_ref[2:3, :]
-    gain_two, shift_two = vec_ref[3:4, :], vec_ref[4:5, :]
+    gain_one, shift_one, down_bias = vec_ref[3:4, :], vec_ref[4:5, :], vec_ref[5:6, :]
+    gain_two, shift_two = vec_ref[6:7, :], vec_ref[7:8, :]
 
     def blocks(body):
         @pl.loop(0, rows, step=BLOCK)
@@ -158,7 +392,7 @@
     @pl.when(phase == 0)
     def _():
         def forward(r, here):
-            pre = dot_nn(hlow[here, :], wu_ref[0]) + ub_ref[0]
+            pre = dot_nn(hlow[here, :], wu_ref[0]) + vec_ref[pl.ds(8 + t, 1), :]
             phi = 0.5 * (1.0 + lax.erf(pre * (0.5**0.5)))
             low = (pre * phi).astype(BF16)
             act[t, here, :] = low
@@ -341,11 +575,26 @@
     )
 
 
+def attend_outs(groups, rows, width):
+    cols = width // groups
+    wide = (groups, rows, WIDE)
+    specs = [
+        result((rows, width)),
+        per_step(wide), per_step(wide), per_step(wide),
+        per_step((groups, rows, cols)), per_step((groups, rows, 128)),
+    ]
+    shapes = [
+        struct((rows, width), F32),
+        struct(wide, BF16), struct(wide, BF16), struct(wide, BF16),
+        struct((groups, rows, cols), BF16), struct((groups, rows, 128), F32),
+    ]
+    return specs, shapes
+
+
 def run_attend(length, tokens, w_attn, bias, out_bias):
     rows, width = tokens.shape
     groups = w_attn.shape[0]
-    cols = width // groups
-    wide = (groups, rows, WIDE)
+    specs, shapes = attend_outs(groups, rows, width)
     return pl.pallas_call(
         attend_kernel,
         grid=(groups,),
@@ -353,25 +602,53 @@
             pl.BlockSpec(memory_space=pltpu.SMEM),
             resident((rows, width)),
             per_step(w_attn.shape),
-            per_step(bias.shape),
+            resident(bias.shape),
             resident(out_bias.shape),
         ],
-        out_specs=[
-            result((rows, width)),
-            per_step(wide), per_step(wide), per_step(wide),
-            per_step((groups, rows, cols)), per_step((groups, rows, 128)),
-        ],
-        out_shape=[
-            struct((rows, width), F32),
-            struct(wide, BF16), struct(wide, BF16), struct(wide, BF16),
-            struct((groups, rows, cols), BF16), struct((groups, rows, 128), F32),
-        ],
+        out_specs=specs,
+        out_shape=shapes,
         compiler_params=params(1),
         name="attend",
     )(length, tokens, w_attn, bias, out_bias)
 
 
-def run_ffn(length, residual, cotangent, vectors, up_bias, w_up, w_down):
+def run_attend_spread(lengths, tokens, vec, w_attn, w_up, w_down):
+    rows, width = tokens.shape
+    groups = 4
+    specs, shapes = attend_outs(groups, rows, width)
+    whole = (2, 2, DEPTH, 2)
+    slab = (groups, width, width)
+    table = segment_tables()
+    return pl.pallas_call(
+        attend_spread_kernel,
+        grid=(groups,),
+        in_specs=[
+            pl.BlockSpec(memory_space=pltpu.SMEM), resident(table.shape), resident((rows, width)),
+            resident(vec.shape), resident(w_attn.shape), resident(w_up.shape), resident(w_down.shape),
+        ],
+        out_specs=specs + [
+            per_step(slab), result((16, width)),
+            pl.BlockSpec(memory_space=pl.ANY), pl.BlockSpec(memory_space=pl.ANY),
+        ],
+        out_shape=shapes + [
+            struct(slab, BF16), struct((16, width), F32),
+            struct((*whole, *w_up.shape), BF16), struct((*whole, *w_down.shape), BF16),
+        ],
+        scratch_shapes=[
+            pltpu.VMEM((*whole, *vec.shape), F32), pltpu.VMEM((*whole, *w_attn.shape), BF16),
+            pltpu.VMEM((groups, 8, 3 * width // groups), F32),
+            pltpu.SemaphoreType.DMA((4, SLOTS)), pltpu.SemaphoreType.DMA((4, SLOTS)),
+            pltpu.SemaphoreType.DMA((4,)),
+        ],
+        compiler_params=pltpu.CompilerParams(
+            dimension_semantics=("arbitrary",), vmem_limit_bytes=VMEM_LIMIT, collective_id=0,
+            has_side_effects=True,
+        ),
+        name="attend",
+    )(lengths, table, tokens, vec, w_attn, w_up, w_down)
+
+
+def run_ffn(length, residual, cotangent, vectors, w_up, w_down):
     rows, width = residual.shape
     groups = w_up.shape[0]
     units = w_up.shape[2]
@@ -385,7 +662,6 @@
             resident((rows, width)),
             resident((rows, width)),
             resident(vectors.shape),
-            pl.BlockSpec((1, 1, units), lambda p, t: (t, 0, 0)),
             slab, slab,
         ],
         out_specs=[
@@ -405,7 +681,7 @@
         ],
         compiler_params=params(2),
         name="ffn",
-    )(length, residual, cotangent, vectors, up_bias, w_up, w_down)
+    )(length, residual, cotangent, vectors, w_up, w_down)
 
 
 def run_attend_back(tokens, w_attn, grad_attn, grad_first, q, k, v, mixed, lse):
@@ -450,31 +726,43 @@
     length = lax.dynamic_slice_in_dim(lengths, rank, 1)
     both = ("dp", "tensor")
 
-    pack = jnp.concatenate([w_query, w_key, w_value, w_out.T, w_up, w_down.T], axis=1)
-    whole = lax.all_gather(pack, both, axis=0, tiled=True)
-    whole = whole.reshape(spans, groups, *pack.shape).swapaxes(0, 1)
-    whole = whole.reshape(groups, width, pack.shape[1])
     cols = width // groups
     units = w_up.shape[1]
-    w_attn, w_in, w_back = whole[:, :, : 4 * cols], whole[:, :, 4 * cols : 4 * cols + units], whole[:, :, 4 * cols + units :]
-
+    count = query_bias.shape[0]
     vectors = (query_bias, value_bias, out_bias, attn_gain, attn_shift, down_bias, ffn_gain, ffn_shift)
-    count = query_bias.shape[0]
-    flat = jnp.concatenate([jnp.stack(vectors).reshape(-1), up_bias])
-    gathered = lax.all_gather(flat, both, axis=0, tiled=True).reshape(spans * groups, -1)
-    full = gathered[:, : 8 * count].reshape(-1, 8, count).swapaxes(0, 1).reshape(8, width)
-    ub = gathered[:, 8 * count :].reshape(groups, 1, units)
-    qb, vb = full[0].reshape(groups, 1, cols), full[1].reshape(groups, 1, cols)
-    bias = jnp.concatenate([qb, jnp.zeros_like(qb), vb], axis=2)
-
-    residual, q, k, v, mixed, lse = run_attend(length, tokens, w_attn, bias, full[2:3])
+    flat = jnp.concatenate([*vectors, up_bias])
+    own_attn = jnp.concatenate([w_query, w_key, w_value, w_out.T], axis=1)
+
+    near = (spans, groups, width, units) == (8, 4, 768, 768)
+    if near:
+        vec = jnp.pad(flat[None], ((0, 7), (0, 384 - flat.shape[0])))
+        residual, q, k, v, mixed, lse, w_attn, full, w_in, w_back = run_attend_spread(
+            lengths, tokens, vec, own_attn, w_up, w_down.T
+        )
+        w_in, w_back = w_in.reshape(groups, width, units), w_back.reshape(groups, width, units)
+    else:
+        pack = jnp.concatenate([own_attn, w_up, w_down.T], axis=1)
+        whole = lax.all_gather(pack, both, axis=0, tiled=True)
+        whole = whole.reshape(spans, groups, *pack.shape).swapaxes(0, 1)
+        whole = whole.reshape(groups, width, pack.shape[1])
+        w_attn, w_in, w_back = jnp.split(whole, [4 * cols, 4 * cols + units], axis=2)
+        gathered = lax.all_gather(flat, both, axis=0, tiled=True).reshape(spans * groups, -1)
+        full = gathered[:, : 8 * count].reshape(-1, 8, count).swapaxes(0, 1).reshape(8, width)
+        full = jnp.concatenate([full, gathered[:, 8 * count :].reshape(groups, units)])
+        full = jnp.pad(full, ((0, 16 - full.shape[0]), (0, 0)))
+        qb, vb = full[0].reshape(groups, 1, cols), full[1].reshape(groups, 1, cols)
+        bias = jnp.pad(jnp.concatenate([qb, jnp.zeros_like(qb), vb], axis=2), ((0, 0), (0, 7), (0, 0)))
+        residual, q, k, v, mixed, lse = run_attend(length, tokens, w_attn, bias, full[2:3])
     output, grad_first, grad_attn, small, grad_in, grad_back = run_ffn(
-        length, residual, cotangent, full[3:8], ub, w_in, w_back
+        length, residual, cotangent, full, w_in, w_back
     )
     grad_tokens, grad_attn_w, bias_grad = run_attend_back(
         tokens, w_attn, grad_attn, grad_first, q, k, v, mixed, lse
     )
 
+    if near:
+        mine = jnp.arange(groups) ^ rank
+        grad_attn_w, bias_grad = grad_attn_w[mine], bias_grad[mine]
     every = jnp.concatenate([grad_attn_w, grad_in, grad_back], axis=2)
     every = every.reshape(groups, spans, width // spans, -1).swapaxes(0, 1)
     every = every.reshape(spans * groups * (width // spans), -1)

time: 494 us -> 441 us (0.89)
  waiting for transfers between devices: 176 us -> 117 us
  Pallas kernels: 177 us -> 232 us
  blocking collectives: 82.1 us -> 44.3 us
  local copies, waits for them, and re-layouts: 34.1 us -> 23.5 us
    all_gather x1 -> x0, waiting for transfers between devices: 57.9 us -> none  [shards(): whole = lax.all_gather(pack, both, axis=0, tiled=True)]
    pallas_call x1, Pallas kernels: 39 us -> 94.7 us  [run_attend_spread(): pl.pallas_call(attend_spread_kernel, grid=(groups,), in_specs=[pl.BlockSp...]
    unnamed x2 -> x1, blocking collectives: 82.1 us -> 44.3 us
    reshape x5 -> x0, local copies, waits for them, and re-layouts: 7.75 us -> none  [the longest x1 6.8 us: shards(): whole = whole.reshape(spans, groups, *pack.shape).swapaxes(0, 1)]
    slice x8 -> x0, local copies, waits for them, and re-layouts: 7.17 us -> none  [the longest x1 5.55 us: shards(): whole[:, :, 4 * cols + units:]]
    gather x0 -> x2, local copies, waits for them, and re-layouts: none -> 5.98 us  [shards(): grad_attn_w, bias_grad = (grad_attn_w[mine], bias_grad[mine])]
  transfers between devices with their start and end apart: 2 -> 1, of which waited for: 2 -> 1; matrix products, arithmetic and copies ran while one was open for 2% -> 1% of each run, Pallas kernels for 0% -> 0%
where the time goes in v2:
time: 441 us
  Pallas kernels  232 us (53%)
  waiting for transfers between devices  117 us (27%)
  blocking collectives  44.3 us (10%)
  local copies, waits for them, and re-layouts  23.5 us (5%)
  between operations  14.2 us (3%)
  other arithmetic  9.85 us (2%)
    reduce_scatter x1, waiting for transfers between devices, shards(): lax.psum_scatter(every, both, scatter_dimension=0, tiled=True).astype(F32)  117 us
    pallas_call x1, Pallas kernels, run_attend_spread(): pl.pallas_call(attend_spread_kernel, grid=(groups,), in_specs=[pl.BlockSp...  94.7 us
    pallas_call x1, Pallas kernels, run_attend_back(): pl.pallas_call(attend_back_kernel, grid=(groups,), in_specs=[resident((ro...  76.7 us
    pallas_call x1, Pallas kernels, run_ffn(): pl.pallas_call(ffn_kernel, grid=(2, groups), in_specs=[pl.BlockSpec(memor...  60.5 us
    unnamed x1, blocking collectives  44.3 us
  transfers between devices with their start and end apart: 1, of which 1 were waited for; matrix products, arithmetic and copies ran while one was open for 1% of the time, Pallas kernels for 0%

profile of v2, /device:TPU:0, one launch (start us, length us, event | category | flops | bytes accessed | tf_op | source)
XLA Modules:
  0.0 440.9 jit_solution(12033415278868913330)
XLA Ops:
  7.3 0.9 copy.42
  8.2 0.9 concatenate.26
  9.1 0.6 pad.4.own_vec
  9.7 1.2 dynamic_slice.3.len_ref
  10.9 1.6 pad_maximum_fusion.1.own_attn
  12.5 0.6 concatenate.25.tab_ref
  13.2 94.7 %attend.1 = (f32[1024,768]{1,0:T(8,128)}, bf16[4,1024,256]{2,1,0:T(8,128)(2,1)}, bf16[4,1024,256]{2,1,0:T(8,128)(2,1)}, bf16[4,1024,256]{2,1,0:T(8,128)(2,1)}, b...) custom-call(s32[4]{0:T(128)} %len_ref.1, ...), custom_call_target="tpu_custom_call" | custom-call | tf_op jit(solution)/shard_map/attend/pallas_call | solution.py:622
  107.8 60.5 %ffn.1 = (f32[1024,768]{1,0:T(8,128)}, f32[1024,768]{1,0:T(8,128)}, bf16[1024,768]{1,0:T(8,128)(2,1)}, f32[16,768]{1,0:T(8,128)}, bf16[4,768,768]{2,1,0:T(8,128)(2,1)}, /*index=5*/bf16[4,768,768]{2,1,0:T(8,128)(2,1)}) custom-call(s32[1]{0:T(128)} %dynamic_slice.3.len_ref, f32[1024,768]{1,0:T(8,128)} %get-tuple-element.36.res_ref, bf16[1024,768]{1,0:T(8,128)(2,1)} %cot_ref.1, ...), custom_call_target="tpu_custom_call" | custom-call | tf_op jit(solution)/shard_map/ffn/pallas_call | solution.py:657
  168.3 76.7 %attend_back.1 = (f32[1024,768]{1,0:T(8,128)}, bf16[4,768,768]{2,1,0:T(8,128)(2,1)}, f32[4,8,192]{2,1,0:T(8,128)}) custom-call(bf16[1024,768]{1,0:T(8,128)(2,1)} %x_ref.3, bf16[4,768,768]{2,1,0:T(8,128)(2,1)} %get-tuple-element.41.w_ref, bf16[1024,768]{1,0:T(8,128)(2,1)} %get-tuple-element.42.gattn_ref, f32[1024,768]{1,0:T(8,128)} %get-tuple-element.43.gfirst_ref, ...), custom_call_target="tpu_custom_call" | custom-call | tf_op jit(solution)/shard_map/attend_back/pallas_call | solution.py:692
  245.0 5.4 %gather_fusion = bf16[4,768,768]{2,1,0:T(8,128)(2,1)} fusion(bf16[4,768,768]{2,1,0:T(8,128)(2,1)} %get-tuple-element.50, s32[1024]{0:T(1024)S(1)} %pad_clamp_fusion), kind=kCustom, calls=%fused_computation | custom fusion | bytes 9437200 | tf_op jit(solution)/shard_map/gather | solution.py:765
  250.5 7.0 %pad_maximum_fusion = bf16[4,768,2304]{2,1,0:T(8,128)(2,1)S(1)} fusion(bf16[4,768,768]{2,1,0:T(8,128)(2,1)} %get-tuple-element.52, bf16[4,768,768]{2,1,0:T(8,128)(2,1)} %get-tuple-element.51, bf16[4,768,768]{2,1,0:T(8,128)(2,1)} %gather_fusion), kind=kLoop, calls=%fused_computation.2 | loop fusion | flops 42467328 | bytes 28311552 | tf_op jit(solution)/shard_map/concatenate | solution.py:766
  257.5 5.7 %copy.43 = bf16[8,4,96,2304]{3,2,1,0:T(8,128)(2,1)} copy(bf16[8,4,96,2304]{3,2,0,1:T(8,128)(2,1)S(1)} %bitcast.17) | data formatting | bytes 28311552 | tf_op jit(solution)/shard_map/transpose | solution.py:767
  263.3 0.8 copy-done.1
  264.1 0.6 gather_fusion.1
  264.7 0.1 concatenate.29
  264.8 0.1 concatenate.31
  264.9 0.1 copy.44
  265.0 0.1 reshape.183
  265.1 0.1 reshape.184
  265.2 0.1 pad_maximum_fusion.2
  265.3 0.1 reshape.185
  265.4 44.3 %all-reduce.1 = f32[9216]{0:T(1024)S(1)} all-reduce(f32[9216]{0:T(1024)S(1)} %reshape.185), channel_id=3, replica_groups=mesh['dp'=8,'tensor'=4] {'dp','tensor'}, use_global_device_ids=true, to_apply=%region_1.2.clone | all-reduce | flops 9216 | bytes 73728
  309.7 0.1 dynamic-slice
  309.8 0.6 slice.89
  310.3 0.6 fusion.2
  311.0 117.2 %reduce-scatter.2.cloned.1.call-done = bf16[96,2304]{1,0:T(8,128)(2,1)} async-done(((bf16[3072,2304]{1,0:T(8,128)(2,1)}), bf16[96,2304]{1,0:T(8,128)(2,1)}) %reduce-scatter.2.cloned.1.call-update) | async-done | bytes 442384 | tf_op jit(solution)/shard_map/reduce_scatter | solution.py:769
  428.1 1.1 convert_element_type.5
  429.2 0.7 slice_bitcast_fusion
  429.9 0.1 slice_bitcast_fusion.1
  430.0 0.7 copy.45
  430.8 1.6 fusion.1
  432.4 1.6 slice.101
  (16 shorter events, 0.2 us)
Async XLA Ops:
  7.2 420.9 %reduce-scatter.2.cloned.1.call-start = ((), (), s32[]{:S(2)}) async-start(), calls=%async_computation.1 | async-start | bytes 14598144 | tf_op jit(solution)/shard_map/reduce_scatter | solution.py:769
  263.3 0.8 copy-start.1
  263.3 0.8 copy-start
Sparse Core Ops, SparseCore 0:
  263.4 164.6 reduce-scatter.1

commit v3 on v2

--- a/solution.py
+++ b/solution.py
@@ -182,6 +182,111 @@
             self.copy(ref, ref, slot, device).wait_send()
 
 
+class Collect:
+    def __init__(self, place, near, far, rc, rb, ra, rz, send, recv, last):
+        self.p, self.near, self.far, self.last = place, near, far, last
+        self.rc, self.rb, self.ra, self.rz, self.send, self.recv = rc, rb, ra, rz, send, recv
+        to_x, to_y = place.device(x=1 - place.x), place.device(y=1 - place.y)
+        self.to_a, self.to_b = (to_x, to_y) if last == "x" else (to_y, to_x)
+        self.to_c = place.device(c=1 - place.c)
+
+    def copy(self, src, dst, slot, device):
+        return pltpu.make_async_remote_copy(
+            src_ref=src, dst_ref=dst, send_sem=self.send.at[slot], recv_sem=self.recv.at[slot],
+            device_id=device, device_id_type=MESH,
+        )
+
+    def copy_c(self, src, dy):
+        return self.copy(src, self.rc.at[dy], dy, self.to_c)
+
+    def copies_b(self):
+        if self.last == "x":
+            return [self.copy(self.far, self.rb, 2, self.to_b)]
+        there = (slice(None), 1 - self.p.x)
+        return [
+            self.copy(part.at[there], self.rb.at[dy], 2 + 5 * dy, self.to_b)
+            for dy, part in enumerate((self.near, self.far))
+        ]
+
+    def copy_a(self):
+        if self.last == "x":
+            return self.copy(self.near.at[:, 1 - self.p.x], self.ra, 3, self.to_a)
+        return self.copy(self.far.at[:, self.p.x], self.ra, 3, self.to_a)
+
+    def copies_z(self):
+        p = self.p
+        return [
+            self.copy(
+                self.near.at[around(p.z, k), p.x], self.rz.at[k - 1], 3 + k, p.device(z=around(p.z, k))
+            )
+            for k in range(1, DEPTH)
+        ]
+
+    def wait_c(self, dy):
+        self.copy_c(self.rc.at[dy], dy).wait_recv()
+
+    def wait_b(self):
+        for copy in self.copies_b():
+            copy.wait_recv()
+
+    def sum_c(self):
+        for dy, part in enumerate((self.near, self.far)):
+            self.wait_c(dy)
+
+            @pl.loop(0, DEPTH)
+            def _(z):
+                part[z] = add(part[z], self.rc[dy, z]).astype(part.dtype)
+
+    def send_b(self):
+        for copy in self.copies_b():
+            copy.start()
+
+    def sum_b(self):
+        self.wait_b()
+        x = self.p.x
+
+        @pl.loop(0, DEPTH)
+        def _(z):
+            if self.last == "x":
+                self.near[z] = add(self.near[z], self.rb[z]).astype(self.near.dtype)
+            else:
+                for dy, part in enumerate((self.near, self.far)):
+                    part[z, x] = add(part[z, x], self.rb[dy, z]).astype(part.dtype)
+
+    def send_a(self):
+        self.copy_a().start()
+
+    def sum_a(self):
+        self.copy_a().wait_recv()
+        x = self.p.x
+
+        @pl.loop(0, DEPTH)
+        def _(z):
+            self.near[z, x] = add(self.near[z, x], self.ra[z]).astype(self.near.dtype)
+
+    def send_z(self):
+        for copy in self.copies_z():
+            copy.start()
+
+    def sum_z(self, out_ref):
+        for copy in self.copies_z():
+            copy.wait_recv()
+        total = self.near[self.p.z, self.p.x].astype(F32)
+        for k in range(DEPTH - 1):
+            total = total + self.rz[k].astype(F32)
+        out_ref[...] = total
+
+    def finish(self):
+        for dy in range(2):
+            self.copy_c(self.rc.at[dy], dy).wait_send()
+        for copy in [*self.copies_b(), self.copy_a(), *self.copies_z()]:
+            copy.wait_send()
+
+
+def add(a, b):
+    return a.astype(F32) + b.astype(F32)
+
+
 def segment_tables():
     lane = jnp.arange(768, dtype=jnp.int32)
     rows = jnp.stack([lane % 24, lane // 24, lane % 96, lane // 96])
@@ -211,6 +316,30 @@
         keep = owner == tab_ref[3:4, :] + 8 * k
         vec_ref[8 + k : 9 + k, :] = jnp.sum(jnp.where(keep, got, 0.0), axis=0, keepdims=True)
     vec_ref[12:, :] = jnp.zeros((vec_ref.shape[0] - 12, width), F32)
+
+
+def cut_vectors(eight, up_rows, tab_ref, out_ref):
+    width = tab_ref.shape[1]
+
+    def owners(shape, dim):
+        p = lax.broadcasted_iota(jnp.int32, shape, dim)
+        return lax.shift_left(p & 7, 2) + lax.shift_right_logical(p, 3)
+
+    def pick(values, table):
+        hot = one_hot(tab_ref, table, 0, 128)
+        return sum(dot_nt(part.astype(BF16), hot) for part in split_three(values))
+
+    both = jnp.concatenate([eight, jnp.zeros_like(eight)], axis=0)
+    keep = owners((32, 16, width), 0) == tab_ref[1:2, :][None]
+    spread = jnp.where(keep, jnp.broadcast_to(both[None], (32, 16, width)), 0.0)
+    blocks = pick(spread.reshape(512, width), 0).reshape(32, 16, 128)
+    owner = owners((32, width), 0)
+    ups = jnp.zeros((32, width), F32)
+    for k in range(4):
+        ups = jnp.where(owner == tab_ref[3:4, :] + 8 * k, up_rows[k : k + 1, :], ups)
+    ups = jnp.broadcast_to(pick(ups, 2)[:, None, :], (32, 16, 128))
+    blocks = jnp.where(lax.broadcasted_iota(jnp.int32, (32, 16, 128), 1) == 8, ups, blocks)
+    out_ref[...] = blocks.reshape(out_ref.shape)
 
 
 def attend_steps(
@@ -461,10 +590,10 @@
         blocks(finish)
 
 
-def attend_back_kernel(
-    x_ref, w_ref, gattn_ref, gfirst_ref, q_ref, k_ref, v_ref, mix_ref, lse_ref,
-    gtok_ref, grad_ref, bias_ref,
-    qh, gh, dq, kh, ds, dqkv,
+def attend_back_steps(
+    hook, before_grads, put_grads,
+    x_ref, w_ref, gattn_ref, gfirst_ref, q_ref, k_ref, v_ref, mix_ref, lse_ref, gtok_ref, bias_ref,
+    qh, gh, dq, kh, dqkv,
 ):
     t = pl.program_id(0)
     rows, width = x_ref.shape
@@ -505,6 +634,7 @@
     @pl.loop(0, rows, step=BLOCK)
     def _(r):
         r = pl.multiple_of(r, BLOCK)
+        hook(r)
         here = pl.ds(r, BLOCK)
         key, value = k_ref[0, here, :], v_ref[0, here, :]
         grad_key = jnp.zeros((BLOCK, WIDE), F32)
@@ -545,12 +675,185 @@
         bias_ref[0, 0:1, :] += jnp.sum(low.astype(F32), axis=0, keepdims=True)
         gtok_ref[here, :] += dot_nt(dqkv[here, :], w_ref[0, :, : 3 * cols])
 
-    @pl.loop(0, width, step=BLOCK)
+    before_grads()
+    half = width // 2
+
+    @pl.loop(0, width, step=half)
     def _(c):
-        c = pl.multiple_of(c, BLOCK)
-        here = pl.ds(c, BLOCK)
-        grad_ref[0, here, : 3 * cols] = dot_tn(x_ref[:, here], dqkv[...]).astype(BF16)
-        grad_ref[0, here, 3 * cols :] = dot_tn(gattn_ref[:, here], mix_ref[0]).astype(BF16)
+        c = pl.multiple_of(c, half)
+        here = pl.ds(c, half)
+        put_grads(c, dot_tn(x_ref[:, here], dqkv[...]), dot_tn(gattn_ref[:, here], mix_ref[0]))
+
+
+def attend_back_kernel(
+    x_ref, w_ref, gattn_ref, gfirst_ref, q_ref, k_ref, v_ref, mix_ref, lse_ref,
+    gtok_ref, grad_ref, bias_ref,
+    *scratch,
+):
+    wide = 3 * mix_ref.shape[2]
+
+    def put(c, qkv, out):
+        here = pl.ds(c, qkv.shape[0])
+        grad_ref[0, here, :wide] = qkv.astype(BF16)
+        grad_ref[0, here, wide:] = out.astype(BF16)
+
+    attend_back_steps(
+        lambda r: None, lambda: None, put,
+        x_ref, w_ref, gattn_ref, gfirst_ref, q_ref, k_ref, v_ref, mix_ref, lse_ref, gtok_ref, bias_ref,
+        *scratch,
+    )
+
+
+def attend_back_collect_kernel(
+    tab_ref, x_ref, w_ref, gattn_ref, gfirst_ref, q_ref, k_ref, v_ref, mix_ref, lse_ref, vec_ref,
+    gup_ref, gdn_ref,
+    gtok_ref, attn_out, up_out, down_out, small_out,
+    qh, gh, dq, kh, dqkv, bias_ref, bias_all,
+    gs, attn_rc, attn_rb, attn_ra, attn_rz,
+    up_acc, up_rc, up_rb, up_ra, up_rz,
+    down_acc, down_rc, down_rb, down_ra, down_rz,
+    small_src, small_acc, small_rc, small_rb, small_ra, small_rz,
+    send, recv, home,
+):
+    t = pl.program_id(0)
+    last = pl.num_programs(0) - 1
+    place = Place()
+    cols = mix_ref.shape[2]
+    wide = 3 * cols
+
+    def collect(n, near, far, rc, rb, ra, rz, axis):
+        return Collect(place, near, far, rc, rb, ra, rz, send.at[n], recv.at[n], axis)
+
+    attn = collect(0, gs.at[3], gs.at[1], attn_rc, attn_rb, attn_ra, attn_rz, "x")
+    up = collect(1, up_acc.at[0], up_acc.at[1], up_rc, up_rb, up_ra, up_rz, "x")
+    down = collect(2, down_acc.at[0], down_acc.at[1], down_rc, down_rb, down_ra, down_rz, "y")
+    small = collect(3, small_acc.at[0], small_acc.at[1], small_rc, small_rb, small_ra, small_rz, "x")
+    rows_y = (place.y, 1 - place.y)
+
+    def homes(src, acc, n):
+        return [
+            pltpu.make_async_copy(src.at[y, place.c], acc.at[dy], home.at[n, dy])
+            for dy, y in enumerate(rows_y)
+        ]
+
+    def begin(piece, src, acc, n):
+        for copy in homes(src, acc, n):
+            copy.start()
+        for dy, y in enumerate(rows_y):
+            piece.copy_c(src.at[y, 1 - place.c], dy).start()
+
+    def settle(src, acc, n):
+        for copy in homes(src, acc, n):
+            copy.wait()
+
+    @pl.when(t == 0)
+    def _():
+        place.greet()
+        begin(up, gup_ref, up_acc, 0)
+        begin(down, gdn_ref, down_acc, 1)
+        settle(gup_ref, up_acc, 0)
+        settle(gdn_ref, down_acc, 1)
+
+    @pl.when(t == 1)
+    def _():
+        down.send_b()
+        attn.copy_c(gs.at[0], 1).start()
+
+    @pl.when(t == 2)
+    def _():
+        down.sum_b()
+
+    @pl.when(t == 3)
+    def _():
+        up.send_z()
+        attn.copy_c(gs.at[2], 0).start()
+
+    def hook(r):
+        def at(step, block, *events):
+            @pl.when((t == step) & (r == block * BLOCK))
+            def _():
+                for event in events:
+                    event()
+
+        at(0, 1, up.sum_c)
+        at(0, 2, up.send_b)
+        at(0, 3, down.sum_c)
+        at(1, 3, up.sum_b)
+        at(2, 0, up.send_a, down.send_a, attn.send_b)
+        at(2, 3, up.sum_a)
+        at(3, 1, down.sum_a)
+        at(3, 2, down.send_z)
+
+    g = place.group(last - t)
+
+    def before_grads():
+        bias_all[g] = bias_ref[0]
+
+        @pl.when(t == 1)
+        def _():
+            attn.wait_c(1)
+
+        @pl.when(t == last)
+        def _():
+            lines = [
+                jnp.concatenate([bias_all[n, row : row + 1, :] for n in range(bias_all.shape[0])], axis=1)
+                for row in range(2)
+            ]
+            cut_vectors(jnp.concatenate([*lines, vec_ref[0:6, :]], axis=0), vec_ref[8:12, :], tab_ref, small_src)
+            attn.wait_c(0)
+            attn.wait_b()
+            begin(small, small_src, small_acc, 2)
+
+    def put(c, qkv, out):
+        start = lax.div(c, 2 * gs.shape[3])
+        some = pl.ds(start, qkv.shape[0] // (2 * gs.shape[3]))
+        shape = (qkv.shape[0] // (2 * gs.shape[3]), *gs.shape[2:4])
+
+        def store(*more):
+            for lanes, value in ((slice(0, wide), qkv), (slice(wide, None), out)):
+                value = value.reshape(*shape, value.shape[1])
+                for ref in more:
+                    value = value + ref[some, :, :, lanes].astype(F32)
+                gs[t, some, :, :, lanes] = value.astype(BF16)
+
+        @pl.when((t == 0) | (t == 2))
+        def _():
+            store()
+
+        @pl.when(t == 1)
+        def _():
+            store(attn_rc.at[1])
+
+        @pl.when(t == last)
+        def _():
+            store(attn_rc.at[0], attn_rb)
+
+    attend_back_steps(
+        hook, before_grads, put,
+        x_ref, w_ref, gattn_ref, gfirst_ref, q_ref, k_ref, v_ref, mix_ref, lse_ref, gtok_ref, bias_ref,
+        qh, gh, dq, kh, dqkv,
+    )
+
+    @pl.when(t == last)
+    def _():
+        settle(small_src, small_acc, 2)
+        small.sum_c()
+        attn.send_a()
+        up.sum_z(up_out)
+        small.send_b()
+        small.sum_b()
+        down.sum_z(down_out)
+        small.send_a()
+        small.sum_a()
+        attn.sum_a()
+        small.send_z()
+        up.finish()
+        down.finish()
+        attn.send_z()
+        small.sum_z(small_out)
+        small.finish()
+        attn.sum_z(attn_out)
+        attn.finish()
 
 
 def resident(shape):
@@ -684,11 +987,19 @@
     )(length, residual, cotangent, vectors, w_up, w_down)
 
 
+def back_scratch(rows, width, cols):
+    heads = cols // HEAD
+    return [
+        pltpu.VMEM((heads, rows, WIDE), BF16), pltpu.VMEM((heads, rows, WIDE), BF16),
+        pltpu.VMEM((rows, WIDE), F32), pltpu.VMEM((heads, rows, WIDE), BF16),
+        pltpu.VMEM((rows, 3 * cols), BF16),
+    ]
+
+
 def run_attend_back(tokens, w_attn, grad_attn, grad_first, q, k, v, mixed, lse):
     rows, width = tokens.shape
     groups = w_attn.shape[0]
     cols = width // groups
-    heads = cols // HEAD
     return pl.pallas_call(
         attend_back_kernel,
         grid=(groups,),
@@ -702,14 +1013,65 @@
         out_shape=[
             struct((rows, width), F32), struct(w_attn.shape, BF16), struct((groups, 8, cols), F32),
         ],
-        scratch_shapes=[
-            pltpu.VMEM((heads, rows, WIDE), BF16), pltpu.VMEM((heads, rows, WIDE), BF16),
-            pltpu.VMEM((rows, WIDE), F32), pltpu.VMEM((heads, rows, WIDE), BF16),
-            pltpu.VMEM((8, 128), BF16), pltpu.VMEM((rows, 3 * cols), BF16),
-        ],
+        scratch_shapes=back_scratch(rows, width, cols),
         compiler_params=params(1),
         name="attend_back",
     )(tokens, w_attn, grad_attn, grad_first, q, k, v, mixed, lse)
+
+
+def run_attend_back_collect(
+    tokens, w_attn, grad_attn, grad_first, q, k, v, mixed, lse, small, grad_up, grad_down
+):
+    rows, width = tokens.shape
+    groups = w_attn.shape[0]
+    cols = width // groups
+    table = segment_tables()
+
+    def back(shape):
+        return pl.BlockSpec((1, *shape[1:]), lambda t: (groups - 1 - t, 0, 0))
+
+    def buffers(block, dtype, last):
+        chip = (DEPTH, 2, *block)
+        return [
+            pltpu.VMEM((2, *chip), dtype),
+            pltpu.VMEM(chip if last == "x" else (2, DEPTH, *block), dtype),
+            pltpu.VMEM((DEPTH, *block), dtype), pltpu.VMEM((DEPTH - 1, *block), dtype),
+        ]
+
+    part = (width // (2 * DEPTH), width)
+    pair = (2, DEPTH, 2)
+    dots = (16, 128)
+    return pl.pallas_call(
+        attend_back_collect_kernel,
+        grid=(groups,),
+        in_specs=[
+            resident(table.shape), resident((rows, width)), back(w_attn.shape),
+            resident((rows, width)), resident((rows, width)),
+            back(q.shape), back(k.shape), back(v.shape), back(mixed.shape), back(lse.shape),
+            resident(small.shape),
+            pl.BlockSpec(memory_space=pl.ANY), pl.BlockSpec(memory_space=pl.ANY),
+        ],
+        out_specs=[result((rows, width)), result(part), result(part), result(part), result(dots)],
+        out_shape=[
+            struct((rows, width), F32), struct(part, F32), struct(part, F32), struct(part, F32),
+            struct(dots, F32),
+        ],
+        scratch_shapes=[
+            *back_scratch(rows, width, cols),
+            pltpu.VMEM((1, 8, cols), F32), pltpu.VMEM((groups, 8, cols), F32),
+            pltpu.VMEM((groups, DEPTH, 2, *part), BF16), *buffers(part, BF16, "x"),
+            pltpu.VMEM((*pair, *part), BF16), *buffers(part, BF16, "x"),
+            pltpu.VMEM((*pair, *part), BF16), *buffers(part, BF16, "y"),
+            pltpu.VMEM((2, *pair, *dots), F32), pltpu.VMEM((*pair, *dots), F32), *buffers(dots, F32, "x"),
+            pltpu.SemaphoreType.DMA((4, 8)), pltpu.SemaphoreType.DMA((4, 8)),
+            pltpu.SemaphoreType.DMA((3, 2)),
+        ],
+        compiler_params=pltpu.CompilerParams(
+            dimension_semantics=("arbitrary",), vmem_limit_bytes=VMEM_LIMIT, collective_id=1,
+            has_side_effects=True,
+        ),
+        name="attend_back",
+    )(table, tokens, w_attn, grad_attn, grad_first, q, k, v, mixed, lse, small, grad_up, grad_down)
 
 
 def shards(
@@ -756,13 +1118,24 @@
     output, grad_first, grad_attn, small, grad_in, grad_back = run_ffn(
         length, residual, cotangent, full, w_in, w_back
     )
+    if near:
+        split = (2, 2, DEPTH, 2, width // (2 * DEPTH), units)
+        grad_tokens, own_a, own_u, own_d, dots = run_attend_back_collect(
+            tokens, w_attn, grad_attn, grad_first, q, k, v, mixed, lse, small,
+            grad_in.reshape(split), grad_back.reshape(split),
+        )
+        tiny8 = dots[:8, :count]
+        return (
+            output, grad_tokens,
+            own_a[:, :cols], own_a[:, cols : 2 * cols], own_a[:, 2 * cols : 3 * cols], own_a[:, 3 * cols :].T,
+            own_u, own_d.T,
+            tiny8[0], tiny8[1], tiny8[2], tiny8[3], tiny8[4], dots[8, : up_bias.shape[0]],
+            tiny8[5], tiny8[6], tiny8[7],
+        )
     grad_tokens, grad_attn_w, bias_grad = run_attend_back(
         tokens, w_attn, grad_attn, grad_first, q, k, v, mixed, lse
     )
 
-    if near:
-        mine = jnp.arange(groups) ^ rank
-        grad_attn_w, bias_grad = grad_attn_w[mine], bias_grad[mine]
     every = jnp.concatenate([grad_attn_w, grad_in, grad_back], axis=2)
     every = every.reshape(groups, spans, width // spans, -1).swapaxes(0, 1)
     every = every.reshape(spans * groups * (width // spans), -1)

time: 441 us -> 306 us (0.69)
  waiting for transfers between devices: 117 us -> 0 us
  Pallas kernels: 232 us -> 288 us
  blocking collectives: 44.3 us -> 0 us
  between operations: 14.2 us -> 0.7 us
  local copies, waits for them, and re-layouts: 23.5 us -> 14.8 us
  other arithmetic: 9.85 us -> 1.65 us
    reduce_scatter x1 -> x0, waiting for transfers between devices: 117 us -> none  [shards(): lax.psum_scatter(every, both, scatter_dimension=0, tiled=True).astype(F32)]
    pallas_call x1, Pallas kernels: 76.7 us -> 133 us  [run_attend_back_collect(): pl.pallas_call(attend_back_collect_kernel, grid=(groups,), in_specs=[resi...]
    unnamed x1 -> x0, blocking collectives: 44.3 us -> none
    concatenate x2 -> x0, other arithmetic: 7.11 us -> none  [the longest x1 7.03 us: shards(): every = jnp.concatenate([grad_attn_w, grad_in, grad_back], axis=2)]
    gather x2 -> x0, local copies, waits for them, and re-layouts: 5.98 us -> none  [shards(): grad_attn_w, bias_grad = (grad_attn_w[mine], bias_grad[mine])]
    transpose x4 -> x1, local copies, waits for them, and re-layouts: 6.64 us -> 1.84 us  [shards(): own_a[:, 3 * cols:]]
    slice x7 -> x0, local copies, waits for them, and re-layouts: 4.52 us -> none  [the longest x1 1.64 us: shards(): owned[:, 4 * cols:4 * cols + units]]
  transfers between devices with their start and end apart: 1 -> 0, of which waited for: 1 -> 0; matrix products, arithmetic and copies ran while one was open for 1% -> 0% of each run, Pallas kernels for 0% -> 0%
where the time goes in v3:
time: 306 us; the launch traced here: 305 us
  Pallas kernels  288 us (94%)
  local copies, waits for them, and re-layouts  14.8 us (5%)
    pallas_call x1, Pallas kernels, run_attend_back_collect(): pl.pallas_call(attend_back_collect_kernel, grid=(groups,), in_specs=[resi...  133 us
    pallas_call x1, Pallas kernels, run_attend_spread(): pl.pallas_call(attend_spread_kernel, grid=(groups,), in_specs=[pl.BlockSp...  94.7 us
    pallas_call x1, Pallas kernels, run_ffn(): pl.pallas_call(ffn_kernel, grid=(2, groups), in_specs=[pl.BlockSpec(memor...  60.4 us
    unnamed x9, local copies, waits for them, and re-layouts  6.88 us

profile of v3, /device:TPU:0, one launch (start us, length us, event | category | flops | bytes accessed | tf_op | source)
XLA Modules:
  0.0 305.2 jit_solution(17325815406478073285)
XLA Ops:
  0.7 1.2 dynamic_slice.3.len_ref
  1.9 0.9 concatenate.11
  2.8 0.6 pad.4.own_vec
  3.4 0.6 concatenate.10.tab_ref
  4.1 0.9 copy.35
  5.0 1.6 pad_maximum_fusion.own_attn
  6.6 94.7 %attend.1 = (f32[1024,768]{1,0:T(8,128)}, bf16[4,1024,256]{2,1,0:T(8,128)(2,1)}, bf16[4,1024,256]{2,1,0:T(8,128)(2,1)}, bf16[4,1024,256]{2,1,0:T(8,128)(2,1)}, b...) custom-call(s32[4]{0:T(128)} %len_ref.1, ...), custom_call_target="tpu_custom_call" | custom-call | tf_op jit(solution)/shard_map/attend/pallas_call | solution.py:925
  101.3 60.4 %ffn.1 = (f32[1024,768]{1,0:T(8,128)}, f32[1024,768]{1,0:T(8,128)}, bf16[1024,768]{1,0:T(8,128)(2,1)}, f32[16,768]{1,0:T(8,128)}, bf16[4,768,768]{2,1,0:T(8,128)(2,1)}, /*index=5*/bf16[4,768,768]{2,1,0:T(8,128)(2,1)}) custom-call(s32[1]{0:T(128)} %dynamic_slice.3.len_ref, f32[1024,768]{1,0:T(8,128)} %get-tuple-element.38.res_ref, bf16[1024,768]{1,0:T(8,128)(2,1)} %cot_ref.1, ...), custom_call_target="tpu_custom_call" | custom-call | tf_op jit(solution)/shard_map/ffn/pallas_call | solution.py:960
  161.7 133.0 %attend_back.1 = (f32[1024,768]{1,0:T(8,128)}, f32[96,768]{1,0:T(8,128)}, f32[96,768]{1,0:T(8,128)}, f32[96,768]{1,0:T(8,128)}, f32[16,128]{1,0:T(8,128)}) custom-call(s32[8,768]{1,0:T(8,128)} %concatenate.10.tab_ref, bf16[1024,768]{1,0:T(8,128)(2,1)} %x_ref.3, bf16[4,768,768]{2,1,0:T(8,128)(2,1)} %get-tuple-element.43.w_ref, ...), custom_call_target="tpu_custom_call" | custom-call | tf_op jit(solution)/shard_map/attend_back/pallas_call | solution.py:1044
  294.7 1.2 slice_bitcast_fusion.4
  295.9 1.5 slice_bitcast_fusion.1
  297.4 1.8 slice_bitcast_fusion
  299.2 0.7 copy.36
  299.9 0.0 copy-start.1
  299.9 0.0 copy-start
  300.0 3.8 %copy.40 = f32[1024,768]{1,0:T(8,128)} copy(f32[1024,768]{1,0:T(8,128)} %get-tuple-element.110) | data formatting | bytes 6291456
  303.8 0.0 copy-done.1
  303.8 0.7 copy.41
  304.5 0.0 copy-done
  304.5 0.7 copy.42
  (4 shorter events, 0.0 us)
Async XLA Ops:
  299.9 3.8 %copy-start.1 = (f32[96,768]{1,0:T(8,128)S(1)}, f32[96,768]{1,0:T(8,128)}, u32[]{:S(2)}) copy-start(f32[96,768]{1,0:T(8,128)} %get-tuple-element.115) | copy-start | bytes 884740
  299.9 4.5 %copy-start = (f32[96,768]{1,0:T(8,128)S(1)}, f32[96,768]{1,0:T(8,128)}, u32[]{:S(2)}) copy-start(f32[96,768]{1,0:T(8,128)} %get-tuple-element.57) | copy-start | bytes 884740

commit v4 on v3

--- a/solution.py
+++ b/solution.py
@@ -67,11 +67,11 @@
 
 MESH = pl.DeviceIdType.MESH
 DEPTH = 4
-SLOTS = 11
+SLOTS = 14
 
 
 def around(z, k):
-    return lax.rem(z + k, DEPTH)
+    return (z, z + 1 - 2 * lax.rem(z, 2), DEPTH - 1 - z, lax.rem(z + 2, DEPTH))[k]
 
 
 class Place:
@@ -103,83 +103,149 @@
         return y * 2 + c
 
 
-class Spread:
-    def __init__(self, place, own, buf, send, recv, home, first):
-        self.p, self.own, self.buf, self.send, self.recv, self.home = place, own, buf, send, recv, home
-        self.first = first
-        self.to_a = place.device(x=1 - place.x) if first == "x" else place.device(y=1 - place.y)
-        self.to_b = place.device(y=1 - place.y) if first == "x" else place.device(x=1 - place.x)
+def remote(src, dst, send, recv, device):
+    return pltpu.make_async_remote_copy(
+        src_ref=src, dst_ref=dst, send_sem=send, recv_sem=recv, device_id=device, device_id_type=MESH
+    )
+
+
+class Moves:
+    def __init__(self, place, send, recv):
+        self.p, self.send, self.recv = place, send, recv
+        self.to_x, self.to_y = place.device(x=1 - place.x), place.device(y=1 - place.y)
         self.to_c = place.device(c=1 - place.c)
 
-    def at(self, z, a=0, b=0, c=0):
+    def to_z(self, k):
+        return self.p.device(z=around(self.p.z, k))
+
+    def copy(self, src, dst, slot, device):
+        return remote(src, dst, self.send.at[slot], self.recv.at[slot], device)
+
+    def arrive(self, ref, slot, device):
+        self.copy(ref, ref, slot, device).wait_recv()
+
+    def gone(self, ref, slot, device):
+        self.copy(ref, ref, slot, device).wait_send()
+
+
+class Spread(Moves):
+    def __init__(self, place, own, buf, send, recv, home, first, rows=slice(None)):
+        super().__init__(place, send, recv)
+        self.own, self.buf, self.home, self.first, self.rows = own.at[rows], buf, home, first, rows
+        self.to_a, self.to_b = (self.to_x, self.to_y) if first == "x" else (self.to_y, self.to_x)
+
+    def at(self, z, a=0, b=0):
         p = self.p
         dx, dy = (a, b) if self.first == "x" else (b, a)
-        y = p.y if dy == 0 else 1 - p.y
-        x = p.x if dx == 0 else 1 - p.x
-        return self.buf.at[y, p.c if c == 0 else 1 - p.c, z, x]
+        return self.buf.at[p.y if dy == 0 else 1 - p.y, p.c, z, p.x if dx == 0 else 1 - p.x, self.rows]
 
     def chip(self, dy, c=0):
         p = self.p
-        return self.buf.at[p.y if dy == 0 else 1 - p.y, p.c if c == 0 else 1 - p.c]
-
-    def copy(self, src, dst, slot, device):
-        return pltpu.make_async_remote_copy(
-            src_ref=src, dst_ref=dst, send_sem=self.send.at[slot], recv_sem=self.recv.at[slot],
-            device_id=device, device_id_type=MESH,
-        )
-
-    def arrive(self, ref, slot, device):
-        self.copy(ref, ref, slot, device).wait_recv()
+        y = p.y if dy == 0 else 1 - p.y
+        return self.buf.at[y, p.c if c == 0 else 1 - p.c, :, :, self.rows]
 
     def local(self):
         return pltpu.make_async_copy(self.own, self.at(self.p.z), self.home)
 
-    def begin(self):
-        p = self.p
+    def begin_z(self):
+        for k in range(1, DEPTH):
+            self.copy(self.own, self.at(self.p.z), k - 1, self.to_z(k)).start()
+
+    def begin_ab(self):
         self.local().start()
+        self.copy(self.own, self.at(self.p.z), 3, self.to_a).start()
+        self.copy(self.own, self.at(self.p.z), 7, self.to_b).start()
+
+    def after_z(self):
         for k in range(1, DEPTH):
-            self.copy(self.own, self.at(p.z), k - 1, p.device(z=around(p.z, k))).start()
-        self.copy(self.own, self.at(p.z), 3, self.to_a).start()
-
-    def after_z(self):
-        p = self.p
-        for k in range(1, DEPTH):
-            ref = self.at(around(p.z, DEPTH - k))
-            self.arrive(ref, k - 1, p.device(z=around(p.z, k)))
-            self.copy(ref, ref, 3 + DEPTH - k, self.to_a).start()
+            ref = self.at(around(self.p.z, k))
+            self.arrive(ref, k - 1, self.to_z(k))
+            self.copy(ref, ref, 3 + k, self.to_a).start()
+            self.copy(ref, ref, 7 + k, self.to_b).start()
         self.local().wait()
-        ref = self.at(slice(None))
-        self.copy(ref, ref, 7, self.to_b).start()
 
     def after_a(self):
         for k in range(DEPTH):
             self.arrive(self.at(around(self.p.z, k), a=1), 3 + k, self.to_a)
         ref = self.at(slice(None), a=1)
-        self.copy(ref, ref, 8, self.to_b).start()
+        self.copy(ref, ref, 11, self.to_b).start()
         if self.first == "x":
             self.swap(0)
 
     def swap(self, dy):
         ref = self.chip(dy)
-        self.copy(ref, ref, 9 + dy, self.to_c).start()
+        self.copy(ref, ref, 12 + dy, self.to_c).start()
 
     def after_b(self):
-        self.arrive(self.at(slice(None), b=1), 7, self.to_b)
+        for k in range(DEPTH):
+            self.arrive(self.at(around(self.p.z, k), b=1), 7 + k, self.to_b)
         if self.first == "y":
             self.swap(0)
-        self.arrive(self.at(slice(None), a=1, b=1), 8, self.to_b)
+        self.arrive(self.at(slice(None), a=1, b=1), 11, self.to_b)
         self.swap(1)
 
     def after_c(self, dy):
-        self.arrive(self.chip(dy, c=1), 9 + dy, self.to_c)
+        self.arrive(self.chip(dy, c=1), 12 + dy, self.to_c)
+
+    def finish(self):
+        one, column, chip = self.at(self.p.z), self.at(slice(None)), self.chip(0)
+        for k in range(1, DEPTH):
+            self.gone(one, k - 1, self.to_z(k))
+        for k in range(DEPTH):
+            self.gone(one, 3 + k, self.to_a)
+            self.gone(one, 7 + k, self.to_b)
+        self.gone(column, 11, self.to_b)
+        for dy in range(2):
+            self.gone(chip, 12 + dy, self.to_c)
+
+
+class SpreadFlat(Moves):
+    def __init__(self, place, own, buf, send, recv, home, rows=slice(None)):
+        super().__init__(place, send, recv)
+        self.own, self.buf, self.home, self.rows = own.at[rows], buf, home, rows
+
+    def at(self, y=slice(None), z=slice(None), x=slice(None), c=0):
+        return self.buf.at[y, self.p.c if c == 0 else 1 - self.p.c, z, x, self.rows]
+
+    def local(self):
+        p = self.p
+        return pltpu.make_async_copy(self.own, self.at(p.y, p.z, p.x), self.home)
+
+    def begin(self):
+        p = self.p
+        self.local().start()
+        self.copy(self.own, self.at(p.y, p.z, p.x), 0, self.to_y).start()
+
+    def after_y(self):
+        p = self.p
+        self.local().wait()
+        self.arrive(self.at(1 - p.y, p.z, p.x), 0, self.to_y)
+        ref = self.at(z=p.z, x=p.x)
+        self.copy(ref, ref, 1, self.to_x).start()
+
+    def after_x(self):
+        p = self.p
+        self.arrive(self.at(z=p.z, x=1 - p.x), 1, self.to_x)
+        ref = self.at(z=p.z)
+        for k in range(1, DEPTH):
+            self.copy(ref, ref, 1 + k, self.to_z(k)).start()
+
+    def after_z(self):
+        for k in range(1, DEPTH):
+            self.arrive(self.at(z=around(self.p.z, k)), 1 + k, self.to_z(k))
+        ref = self.at()
+        self.copy(ref, ref, 5, self.to_c).start()
+
+    def after_c(self):
+        self.arrive(self.at(c=1), 5, self.to_c)
 
     def finish(self):
         p = self.p
-        one, column, chip = self.at(p.z), self.at(slice(None)), self.chip(0)
-        sizes = [(one, p.device(z=around(p.z, k))) for k in range(1, DEPTH)] + [(one, self.to_a)] * DEPTH
-        sizes += [(column, self.to_b)] * 2 + [(chip, self.to_c)] * 2
-        for slot, (ref, device) in enumerate(sizes):
-            self.copy(ref, ref, slot, device).wait_send()
+        self.gone(self.at(p.y, p.z, p.x), 0, self.to_y)
+        self.gone(self.at(z=p.z, x=p.x), 1, self.to_x)
+        for k in range(1, DEPTH):
+            self.gone(self.at(z=p.z), 1 + k, self.to_z(k))
+        self.gone(self.at(), 5, self.to_c)
 
 
 class Collect:
@@ -283,6 +349,119 @@
             copy.wait_send()
 
 
+class CollectFlat(Moves):
+    def __init__(self, place, acc, rc, rz, rx, ry, send, recv):
+        super().__init__(place, send, recv)
+        self.acc, self.rc, self.rz, self.rx, self.ry = acc, rc, rz, rx, ry
+
+    def copy_c(self, src, dy):
+        return self.copy(src, self.rc.at[dy], dy, self.to_c)
+
+    def copies_z(self):
+        return [
+            self.copy(self.acc.at[:, around(self.p.z, k)], self.rz.at[k - 1], 1 + k, self.to_z(k))
+            for k in range(1, DEPTH)
+        ]
+
+    def copy_x(self):
+        return self.copy(self.acc.at[:, self.p.z, 1 - self.p.x], self.rx, 5, self.to_x)
+
+    def copy_y(self):
+        return self.copy(self.acc.at[1, self.p.z, self.p.x], self.ry, 6, self.to_y)
+
+    def sum_c(self):
+        for dy in range(2):
+            self.copy_c(self.rc.at[dy], dy).wait_recv()
+
+            @pl.loop(0, DEPTH)
+            def _(z):
+                self.acc[dy, z] = add(self.acc[dy, z], self.rc[dy, z]).astype(BF16)
+
+    def send_z(self):
+        for copy in self.copies_z():
+            copy.start()
+
+    def sum_z(self):
+        for copy in self.copies_z():
+            copy.wait_recv()
+        z = self.p.z
+        for dy in range(2):
+            total = add(self.acc[dy, z], self.rz[0, dy])
+            total = total + add(self.rz[1, dy], self.rz[2, dy])
+            self.acc[dy, z] = total.astype(BF16)
+
+    def send_x(self):
+        self.copy_x().start()
+
+    def sum_x(self):
+        self.copy_x().wait_recv()
+        z, x = self.p.z, self.p.x
+        for dy in range(2):
+            self.acc[dy, z, x] = add(self.acc[dy, z, x], self.rx[dy]).astype(BF16)
+
+    def send_y(self):
+        self.copy_y().start()
+
+    def sum_y(self, out_ref):
+        self.copy_y().wait_recv()
+        out_ref[...] = add(self.acc[0, self.p.z, self.p.x], self.ry[...])
+
+    def finish(self):
+        for dy in range(2):
+            self.copy_c(self.rc.at[dy], dy).wait_send()
+        for copy in [*self.copies_z(), self.copy_x(), self.copy_y()]:
+            copy.wait_send()
+
+
+class Tail(Moves):
+    def __init__(self, place, near, rx, rz, sz, sx, send, recv):
+        super().__init__(place, send, recv)
+        self.near, self.rx, self.rz, self.sz, self.sx = near, rx, rz, sz, sx
+        cut = rx.shape[1]
+        self.most, self.others = slice(0, cut), slice(cut, cut + sx.shape[0])
+
+    def first(self):
+        p = self.p
+        copies = [self.copy(self.near.at[:, 1 - p.x, self.most], self.rx, 0, self.to_x)]
+        return copies + [
+            self.copy(self.near.at[around(p.z, k), :, self.others], self.sz.at[k - 1], k, self.to_z(k))
+            for k in range(1, DEPTH)
+        ]
+
+    def second(self):
+        p = self.p
+        copies = [
+            self.copy(self.near.at[around(p.z, k), p.x, self.most], self.rz.at[k - 1], 3 + k, self.to_z(k))
+            for k in range(1, DEPTH)
+        ]
+        return copies + [self.copy(self.near.at[p.z, 1 - p.x, self.others], self.sx, 7, self.to_x)]
+
+    def sum_first(self):
+        for copy in self.first():
+            copy.wait_recv()
+        p = self.p
+
+        @pl.loop(0, DEPTH)
+        def _(z):
+            self.near[z, p.x, self.most] = add(self.near[z, p.x, self.most], self.rx[z]).astype(BF16)
+
+        total = add(self.near[p.z, :, self.others], self.sz[0])
+        total = total + add(self.sz[1], self.sz[2])
+        self.near[p.z, :, self.others] = total.astype(BF16)
+
+    def sum_second(self, out_ref):
+        for copy in self.second():
+            copy.wait_recv()
+        p = self.p
+        total = add(self.near[p.z, p.x, self.most], self.rz[0])
+        out_ref[self.most, :] = total + add(self.rz[1], self.rz[2])
+        out_ref[self.others, :] = add(self.near[p.z, p.x, self.others], self.sx[...])
+
+    def finish(self):
+        for copy in [*self.first(), *self.second()]:
+            copy.wait_send()
+
+
 def add(a, b):
     return a.astype(F32) + b.astype(F32)
 
@@ -297,33 +476,32 @@
     return (row_iota(rows, tab_ref.shape[1]) == start + tab_ref[row : row + 1, :]).astype(BF16)
 
 
+def owners(shape, dim):
+    p = lax.broadcasted_iota(jnp.int32, shape, dim)
+    return lax.shift_left(p & 7, 2) + lax.shift_right_logical(p, 3)
+
+
 def join_vectors(block_ref, tab_ref, vec_ref):
-    pieces = jnp.sum(block_ref[...].reshape(32, 8, 384), axis=1)
-    parts = jnp.concatenate(split_three(pieces), axis=0).astype(BF16)
+    blocks = block_ref[...].reshape(32, 16, 128)
     width = vec_ref.shape[1]
-    row = row_iota(32, width)
-    owner = lax.shift_left(row & 7, 2) + lax.shift_right_logical(row, 3)
-
-    def place(start, table):
-        got = dot_nn(parts, one_hot(tab_ref, table, start, 384))
-        return got[:32] + got[32:64] + got[64:]
-
-    for j in range(8):
-        keep = owner == tab_ref[1:2, :]
-        vec_ref[j : j + 1, :] = jnp.sum(jnp.where(keep, place(24 * j, 0), 0.0), axis=0, keepdims=True)
-    got = place(192, 2)
+
+    def place(values, table):
+        hot = one_hot(tab_ref, table, 0, 128)
+        hi, mid, low = (dot_nn(part.astype(BF16), hot) for part in split_three(values))
+        return hi + mid + low
+
+    keep = owners((32, 16, width), 0) == tab_ref[1:2, :][None]
+    got = place(blocks.reshape(512, 128), 0).reshape(32, 16, width)
+    vec_ref[...] = jnp.sum(jnp.where(keep, got, 0.0), axis=0)
+    row = lax.broadcasted_iota(jnp.int32, (32, 16, 128), 1)
+    got = place(jnp.sum(jnp.where(row == 8, blocks, 0.0), axis=1), 2)
     for k in range(4):
-        keep = owner == tab_ref[3:4, :] + 8 * k
+        keep = owners((32, width), 0) == tab_ref[3:4, :] + 8 * k
         vec_ref[8 + k : 9 + k, :] = jnp.sum(jnp.where(keep, got, 0.0), axis=0, keepdims=True)
-    vec_ref[12:, :] = jnp.zeros((vec_ref.shape[0] - 12, width), F32)
 
 
 def cut_vectors(eight, up_rows, tab_ref, out_ref):
     width = tab_ref.shape[1]
-
-    def owners(shape, dim):
-        p = lax.broadcasted_iota(jnp.int32, shape, dim)
-        return lax.shift_left(p & 7, 2) + lax.shift_right_logical(p, 3)
 
     def pick(values, table):
         hot = one_hot(tab_ref, table, 0, 128)
@@ -412,34 +590,43 @@
     place = Place()
     cols = mix_ref.shape[2]
 
-    def spread(n, own, buf, first):
-        return Spread(place, own, buf, send.at[n], recv.at[n], home.at[n], first)
-
-    small = spread(0, own_vec, vec_buf, "x")
+    def spread(n, own, buf, first, rows=slice(None)):
+        return Spread(place, own, buf, send.at[n], recv.at[n], home.at[n], first, rows)
+
+    def flat(n, own, buf, rows=slice(None)):
+        return SpreadFlat(place, own, buf, send.at[n], recv.at[n], home.at[n], rows)
+
+    cut = own_down.shape[0] * 2 // 3
+    small = flat(0, own_vec, vec_buf)
     attn = spread(1, own_attn, attn_buf, "x")
     up = spread(2, own_up, up_ref, "y")
-    down = spread(3, own_down, down_ref, "x")
+    down = spread(3, own_down, down_ref, "x", slice(0, cut))
+    rest = flat(4, own_down, down_ref, slice(cut, None))
 
     @pl.when(t == 0)
     def _():
         place.greet()
         small.begin()
-        attn.begin()
+        attn.begin_z()
+        small.after_y()
+        small.after_x()
+        attn.begin_ab()
+        rest.begin()
+        down.begin_ab()
+        up.begin_ab()
+        attn.after_z()
+        up.begin_z()
+        down.begin_z()
+        rest.after_y()
         small.after_z()
-        small.after_a()
-        small.after_b()
-        small.after_c(0)
-        small.after_c(1)
+        small.after_c()
         join_vectors(vec_buf, tab_ref, vec_ref)
         for g in range(bias_buf.shape[0]):
             there = slice(g * cols, (g + 1) * cols)
             bias_buf[g, 0:1, :] = jnp.concatenate(
                 [vec_ref[0:1, there], jnp.zeros((1, cols), F32), vec_ref[1:2, there]], axis=1
             )
-        attn.after_z()
         attn.after_a()
-        up.begin()
-        down.begin()
 
     @pl.when(t == 1)
     def _():
@@ -456,11 +643,13 @@
                 for event in events:
                     event()
 
-        at(0, 3, up.after_z)
-        at(1, 1, attn.after_b, down.after_z)
-        at(1, 3, up.after_a)
-        at(2, 2, down.after_a)
-        at(3, 1, up.after_b)
+        at(0, 0, rest.after_x)
+        at(0, 1, up.after_z)
+        at(1, 1, down.after_z)
+        at(1, 2, attn.after_b)
+        at(2, 0, down.after_a)
+        at(2, 1, up.after_a)
+        at(3, 1, rest.after_z)
 
     g = place.group(t)
     y, c = lax.div(g, 2), lax.rem(g, 2)
@@ -477,10 +666,12 @@
     @pl.when(t == pl.num_programs(0) - 1)
     def _():
         down.after_b()
-        for piece in (up, down):
+        up.after_b()
+        rest.after_c()
+        for piece in (down, up):
             piece.after_c(0)
             piece.after_c(1)
-        for piece in (small, attn, up, down):
+        for piece in (small, attn, up, down, rest):
             piece.finish()
 
 
@@ -709,9 +900,10 @@
     gup_ref, gdn_ref,
     gtok_ref, attn_out, up_out, down_out, small_out,
     qh, gh, dq, kh, dqkv, bias_ref, bias_all,
-    gs, attn_rc, attn_rb, attn_ra, attn_rz,
+    gs, attn_rc, attn_rb, tail_rx, tail_rz, tail_sz, tail_sx,
     up_acc, up_rc, up_rb, up_ra, up_rz,
     down_acc, down_rc, down_rb, down_ra, down_rz,
+    rest_acc, rest_rc, rest_rz, rest_rx, rest_ry,
     small_src, small_acc, small_rc, small_rb, small_ra, small_rz,
     send, recv, home,
 ):
@@ -724,49 +916,51 @@
     def collect(n, near, far, rc, rb, ra, rz, axis):
         return Collect(place, near, far, rc, rb, ra, rz, send.at[n], recv.at[n], axis)
 
-    attn = collect(0, gs.at[3], gs.at[1], attn_rc, attn_rb, attn_ra, attn_rz, "x")
+    attn = collect(0, gs.at[3], gs.at[1], attn_rc, attn_rb, None, None, "x")
     up = collect(1, up_acc.at[0], up_acc.at[1], up_rc, up_rb, up_ra, up_rz, "x")
     down = collect(2, down_acc.at[0], down_acc.at[1], down_rc, down_rb, down_ra, down_rz, "y")
     small = collect(3, small_acc.at[0], small_acc.at[1], small_rc, small_rb, small_ra, small_rz, "x")
+    rest = CollectFlat(place, rest_acc, rest_rc, rest_rz, rest_rx, rest_ry, send.at[4], recv.at[4])
+    tail = Tail(place, gs.at[3], tail_rx, tail_rz, tail_sz, tail_sx, send.at[5], recv.at[5])
     rows_y = (place.y, 1 - place.y)
-
-    def homes(src, acc, n):
+    cut = down_acc.shape[3]
+    head, foot = slice(0, cut), slice(cut, cut + rest_acc.shape[3])
+
+    def homes(src, acc, n, rows=slice(None)):
         return [
-            pltpu.make_async_copy(src.at[y, place.c], acc.at[dy], home.at[n, dy])
+            pltpu.make_async_copy(src.at[y, place.c, :, :, rows], acc.at[dy], home.at[n, dy])
             for dy, y in enumerate(rows_y)
         ]
 
-    def begin(piece, src, acc, n):
-        for copy in homes(src, acc, n):
+    def begin(piece, src, acc, n, rows=slice(None)):
+        for dy, y in enumerate(rows_y):
+            piece.copy_c(src.at[y, 1 - place.c, :, :, rows], dy).start()
+        for copy in homes(src, acc, n, rows):
             copy.start()
-        for dy, y in enumerate(rows_y):
-            piece.copy_c(src.at[y, 1 - place.c], dy).start()
-
-    def settle(src, acc, n):
-        for copy in homes(src, acc, n):
+
+    def settle(src, acc, n, rows=slice(None)):
+        for copy in homes(src, acc, n, rows):
             copy.wait()
 
     @pl.when(t == 0)
     def _():
         place.greet()
         begin(up, gup_ref, up_acc, 0)
-        begin(down, gdn_ref, down_acc, 1)
-        settle(gup_ref, up_acc, 0)
-        settle(gdn_ref, down_acc, 1)
+        begin(down, gdn_ref, down_acc, 1, head)
+        begin(rest, gdn_ref, rest_acc, 3, foot)
 
     @pl.when(t == 1)
     def _():
-        down.send_b()
         attn.copy_c(gs.at[0], 1).start()
 
     @pl.when(t == 2)
     def _():
-        down.sum_b()
+        up.sum_b()
 
     @pl.when(t == 3)
     def _():
-        up.send_z()
         attn.copy_c(gs.at[2], 0).start()
+        up.sum_a()
 
     def hook(r):
         def at(step, block, *events):
@@ -775,34 +969,51 @@
                 for event in events:
                     event()
 
-        at(0, 1, up.sum_c)
+        def up_first():
+            settle(gup_ref, up_acc, 0)
+            up.sum_c()
+
+        def down_first():
+            settle(gdn_ref, down_acc, 1, head)
+            settle(gdn_ref, rest_acc, 3, foot)
+            down.sum_c()
+            rest.sum_c()
+
+        at(0, 1, up_first)
         at(0, 2, up.send_b)
-        at(0, 3, down.sum_c)
-        at(1, 3, up.sum_b)
-        at(2, 0, up.send_a, down.send_a, attn.send_b)
-        at(2, 3, up.sum_a)
-        at(3, 1, down.sum_a)
-        at(3, 2, down.send_z)
+        at(0, 3, down_first)
+        at(1, 3, down.sum_b)
+        at(2, 0, up.send_a, attn.send_b)
+        at(2, 1, rest.sum_z)
+        at(2, 2, rest.send_x, down.sum_a)
+        at(2, 3, down.send_z, rest.sum_x)
+        at(3, 0, up.send_z)
+        at(3, 1, lambda: down.sum_z(down_out.at[head]))
+        at(3, 2, lambda: rest.sum_y(down_out.at[foot]))
 
     g = place.group(last - t)
 
     def before_grads():
         bias_all[g] = bias_ref[0]
 
+        @pl.when(t == 0)
+        def _():
+            down.send_b()
+            rest.send_z()
+
         @pl.when(t == 1)
         def _():
+            down.send_a()
             attn.wait_c(1)
+
+        @pl.when(t == 2)
+        def _():
+            rest.send_y()
 
         @pl.when(t == last)
         def _():
-            lines = [
-                jnp.concatenate([bias_all[n, row : row + 1, :] for n in range(bias_all.shape[0])], axis=1)
-                for row in range(2)
-            ]
-            cut_vectors(jnp.concatenate([*lines, vec_ref[0:6, :]], axis=0), vec_ref[8:12, :], tab_ref, small_src)
             attn.wait_c(0)
             attn.wait_b()
-            begin(small, small_src, small_acc, 2)
 
     def put(c, qkv, out):
         start = lax.div(c, 2 * gs.shape[3])
@@ -836,24 +1047,36 @@
 
     @pl.when(t == last)
     def _():
+        up.sum_z(up_out)
+        for copy in tail.first():
+            copy.start()
+        lines = [
+            jnp.concatenate([bias_all[n, row : row + 1, :] for n in range(bias_all.shape[0])], axis=1)
+            for row in range(2)
+        ]
+        cut_vectors(jnp.concatenate([*lines, vec_ref[0:6, :]], axis=0), vec_ref[8:12, :], tab_ref, small_src)
+        begin(small, small_src, small_acc, 2)
         settle(small_src, small_acc, 2)
         small.sum_c()
-        attn.send_a()
-        up.sum_z(up_out)
         small.send_b()
         small.sum_b()
-        down.sum_z(down_out)
         small.send_a()
-        small.sum_a()
-        attn.sum_a()
-        small.send_z()
         up.finish()
         down.finish()
-        attn.send_z()
+        rest.finish()
+        tail.sum_first()
+        small.sum_a()
+        small.send_z()
+        for copy in tail.second():
+            copy.start()
         small.sum_z(small_out)
         small.finish()
-        attn.sum_z(attn_out)
-        attn.finish()
+        for dy in range(2):
+            attn.copy_c(attn_rc.at[dy], dy).wait_send()
+        for copy in attn.copies_b():
+            copy.wait_send()
+        tail.sum_second(attn_out)
+        tail.finish()
 
 
 def resident(shape):
@@ -940,8 +1163,8 @@
         scratch_shapes=[
             pltpu.VMEM((*whole, *vec.shape), F32), pltpu.VMEM((*whole, *w_attn.shape), BF16),
             pltpu.VMEM((groups, 8, 3 * width // groups), F32),
-            pltpu.SemaphoreType.DMA((4, SLOTS)), pltpu.SemaphoreType.DMA((4, SLOTS)),
-            pltpu.SemaphoreType.DMA((4,)),
+            pltpu.SemaphoreType.DMA((5, SLOTS)), pltpu.SemaphoreType.DMA((5, SLOTS)),
+            pltpu.SemaphoreType.DMA((5,)),
         ],
         compiler_params=pltpu.CompilerParams(
             dimension_semantics=("arbitrary",), vmem_limit_bytes=VMEM_LIMIT, collective_id=0,
@@ -1039,6 +1262,7 @@
         ]
 
     part = (width // (2 * DEPTH), width)
+    half, third = (part[0] // 2, width), part[0] // 3
     pair = (2, DEPTH, 2)
     dots = (16, 128)
     return pl.pallas_call(
@@ -1059,12 +1283,16 @@
         scratch_shapes=[
             *back_scratch(rows, width, cols),
             pltpu.VMEM((1, 8, cols), F32), pltpu.VMEM((groups, 8, cols), F32),
-            pltpu.VMEM((groups, DEPTH, 2, *part), BF16), *buffers(part, BF16, "x"),
+            pltpu.VMEM((groups, DEPTH, 2, *part), BF16), *buffers(part, BF16, "x")[:2],
+            pltpu.VMEM((DEPTH, 2 * third, width), BF16), pltpu.VMEM((DEPTH - 1, 2 * third, width), BF16),
+            pltpu.VMEM((DEPTH - 1, 2, third, width), BF16), pltpu.VMEM((third, width), BF16),
             pltpu.VMEM((*pair, *part), BF16), *buffers(part, BF16, "x"),
-            pltpu.VMEM((*pair, *part), BF16), *buffers(part, BF16, "y"),
+            pltpu.VMEM((*pair, *half), BF16), *buffers(half, BF16, "y"),
+            pltpu.VMEM((*pair, *half), BF16), pltpu.VMEM((*pair, *half), BF16),
+            pltpu.VMEM((DEPTH - 1, 2, 2, *half), BF16), pltpu.VMEM((2, *half), BF16), pltpu.VMEM(half, BF16),
             pltpu.VMEM((2, *pair, *dots), F32), pltpu.VMEM((*pair, *dots), F32), *buffers(dots, F32, "x"),
-            pltpu.SemaphoreType.DMA((4, 8)), pltpu.SemaphoreType.DMA((4, 8)),
-            pltpu.SemaphoreType.DMA((3, 2)),
+            pltpu.SemaphoreType.DMA((6, 8)), pltpu.SemaphoreType.DMA((6, 8)),
+            pltpu.SemaphoreType.DMA((4, 2)),
         ],
         compiler_params=pltpu.CompilerParams(
             dimension_semantics=("arbitrary",), vmem_limit_bytes=VMEM_LIMIT, collective_id=1,
@@ -1097,7 +1325,8 @@
 
     near = (spans, groups, width, units) == (8, 4, 768, 768)
     if near:
-        vec = jnp.pad(flat[None], ((0, 7), (0, 384 - flat.shape[0])))
+        vec = jnp.pad(jnp.stack(vectors), ((0, 8), (0, 128 - count)))
+        vec = vec.at[8, : up_bias.shape[0]].set(up_bias)
         residual, q, k, v, mixed, lse, w_attn, full, w_in, w_back = run_attend_spread(
             lengths, tokens, vec, own_attn, w_up, w_down.T
         )

time: 306 us -> 280 us (0.915)
  Pallas kernels: 288 us -> 263 us
    pallas_call x1, Pallas kernels: 133 us -> 115 us  [run_attend_back_collect(): pl.pallas_call(attend_back_collect_kernel, grid=(groups,), in_specs=[resi...]
    pallas_call x1, Pallas kernels: 94.7 us -> 87.1 us  [run_attend_spread(): pl.pallas_call(attend_spread_kernel, grid=(groups,), in_specs=[pl.BlockSp...]
    unnamed x9 -> x11, local copies, waits for them, and re-layouts: 6.88 us -> 6.88 us
where the time goes in v4:
time: 280 us
  Pallas kernels  263 us (94%)
  local copies, waits for them, and re-layouts  14.9 us (5%)
    pallas_call x1, Pallas kernels, run_attend_back_collect(): pl.pallas_call(attend_back_collect_kernel, grid=(groups,), in_specs=[resi...  115 us
    pallas_call x1, Pallas kernels, run_attend_spread(): pl.pallas_call(attend_spread_kernel, grid=(groups,), in_specs=[pl.BlockSp...  87.1 us
    pallas_call x1, Pallas kernels, run_ffn(): pl.pallas_call(ffn_kernel, grid=(2, groups), in_specs=[pl.BlockSpec(memor...  60.4 us
    unnamed x11, local copies, waits for them, and re-layouts  6.88 us

profile of v4, /device:TPU:0, one launch (start us, length us, event | category | flops | bytes accessed | tf_op | source)
XLA Modules:
  0.0 280.0 jit_solution(6774552642579579396)
XLA Ops:
  0.7 1.2 dynamic_slice.3.len_ref
  1.9 0.8 stack.43
  2.7 0.8 scatter.4.own_vec
  3.5 0.0 copy-start.2
  3.6 0.6 concatenate.9.tab_ref
  4.2 0.9 copy.35
  5.1 1.6 pad_maximum_fusion.own_attn
  6.7 0.0 copy-done.2
  6.7 87.1 %attend.1 = (f32[1024,768]{1,0:T(8,128)}, bf16[4,1024,256]{2,1,0:T(8,128)(2,1)}, bf16[4,1024,256]{2,1,0:T(8,128)(2,1)}, bf16[4,1024,256]{2,1,0:T(8,128)(2,1)}, b...) custom-call(s32[4]{0:T(128)} %len_ref.1, ...), custom_call_target="tpu_custom_call" | custom-call | tf_op jit(solution)/shard_map/attend/pallas_call | solution.py:1148
  93.8 60.4 %ffn.1 = (f32[1024,768]{1,0:T(8,128)}, f32[1024,768]{1,0:T(8,128)}, bf16[1024,768]{1,0:T(8,128)(2,1)}, f32[16,768]{1,0:T(8,128)}, bf16[4,768,768]{2,1,0:T(8,128)(2,1)}, /*index=5*/bf16[4,768,768]{2,1,0:T(8,128)(2,1)}) custom-call(s32[1]{0:T(128)} %dynamic_slice.3.len_ref, f32[1024,768]{1,0:T(8,128)} %get-tuple-element.50.res_ref, bf16[1024,768]{1,0:T(8,128)(2,1)} %cot_ref.1, ...), custom_call_target="tpu_custom_call" | custom-call | tf_op jit(solution)/shard_map/ffn/pallas_call | solution.py:1183
  154.2 115.3 %attend_back.1 = (f32[1024,768]{1,0:T(8,128)}, f32[96,768]{1,0:T(8,128)}, f32[96,768]{1,0:T(8,128)}, f32[96,768]{1,0:T(8,128)}, f32[16,128]{1,0:T(8,128)}) custom-call(s32[8,768]{1,0:T(8,128)} %concatenate.9.tab_ref, bf16[1024,768]{1,0:T(8,128)(2,1)} %x_ref.3, bf16[4,768,768]{2,1,0:T(8,128)(2,1)} %get-tuple-element.55.w_ref, ...), custom_call_target="tpu_custom_call" | custom-call | tf_op jit(solution)/shard_map/attend_back/pallas_call | solution.py:1268
  269.5 1.2 slice_bitcast_fusion.4
  270.7 1.5 slice_bitcast_fusion.1
  272.2 1.8 slice_bitcast_fusion
  274.0 0.7 copy.36
  274.8 0.0 copy-start.1
  274.8 0.0 copy-start
  274.8 3.8 %copy.41 = f32[1024,768]{1,0:T(8,128)} copy(f32[1024,768]{1,0:T(8,128)} %get-tuple-element.122) | data formatting | bytes 6291456
  278.6 0.0 copy-done.1
  278.6 0.7 copy.42
  279.3 0.0 copy-done
  279.3 0.7 copy.43
  (4 shorter events, 0.0 us)
Async XLA Ops:
  3.5 3.2 %copy-start.2 = (f32[16,128]{1,0:T(8,128)}, f32[16,128]{1,0:T(8,128)S(1)}, u32[]{:S(2)}) copy-start(f32[16,128]{1,0:T(8,128)S(1)} %scatter.4.own_vec) | copy-start | bytes 24580
  274.8 3.8 %copy-start.1 = (f32[96,768]{1,0:T(8,128)S(1)}, f32[96,768]{1,0:T(8,128)}, u32[]{:S(2)}) copy-start(f32[96,768]{1,0:T(8,128)} %get-tuple-element.127) | copy-start | bytes 884740
  274.8 4.5 %copy-start = (f32[96,768]{1,0:T(8,128)S(1)}, f32[96,768]{1,0:T(8,128)}, u32[]{:S(2)}) copy-start(f32[96,768]{1,0:T(8,128)} %get-tuple-element.69) | copy-start | bytes 884740

commit v5 on v4

--- a/solution.py
+++ b/solution.py
@@ -1,7 +1,6 @@
-import functools
-
 import jax
 import jax.numpy as jnp
+import numpy as np
 from jax import lax
 from jax.experimental import pallas as pl
 from jax.experimental.pallas import tpu as pltpu
@@ -467,9 +466,9 @@
 
 
 def segment_tables():
-    lane = jnp.arange(768, dtype=jnp.int32)
-    rows = jnp.stack([lane % 24, lane // 24, lane % 96, lane // 96])
-    return jnp.concatenate([rows, jnp.zeros_like(rows)])
+    lane = np.arange(768, dtype=np.int32)
+    rows = np.stack([lane % 24, lane // 24, lane % 96, lane // 96])
+    return jnp.asarray(np.concatenate([rows, np.zeros_like(rows)]))
 
 
 def one_hot(tab_ref, row, start, rows):
@@ -534,7 +533,7 @@
             r = pl.multiple_of(r, BLOCK)
             res_ref[pl.ds(r, BLOCK), :] = x_ref[pl.ds(r, BLOCK), :].astype(F32) + out_bias[...]
 
-    @pl.loop(0, rows, step=BLOCK)
+    @pl.loop(0, rows, step=BLOCK, unroll=2)
     def _(r):
         r = pl.multiple_of(r, BLOCK)
         here = pl.ds(r, BLOCK)
@@ -643,13 +642,14 @@
                 for event in events:
                     event()
 
-        at(0, 0, rest.after_x)
-        at(0, 1, up.after_z)
-        at(1, 1, down.after_z)
+        at(0, 2, up.after_z)
+        at(1, 1, down.after_z, rest.after_x)
         at(1, 2, attn.after_b)
         at(2, 0, down.after_a)
         at(2, 1, up.after_a)
         at(3, 1, rest.after_z)
+        at(3, 2, down.after_b)
+        at(3, 3, up.after_b)
 
     g = place.group(t)
     y, c = lax.div(g, 2), lax.rem(g, 2)
@@ -665,8 +665,6 @@
 
     @pl.when(t == pl.num_programs(0) - 1)
     def _():
-        down.after_b()
-        up.after_b()
         rest.after_c()
         for piece in (down, up):
             piece.after_c(0)
@@ -683,12 +681,12 @@
     phase, t = pl.program_id(0), pl.program_id(1)
     last = pl.num_programs(1) - 1
     rows, width = res_ref.shape
-    length = len_ref[0]
+    length = len_ref[lax.axis_index("tensor")]
     gain_one, shift_one, down_bias = vec_ref[3:4, :], vec_ref[4:5, :], vec_ref[5:6, :]
     gain_two, shift_two = vec_ref[6:7, :], vec_ref[7:8, :]
 
     def blocks(body):
-        @pl.loop(0, rows, step=BLOCK)
+        @pl.loop(0, rows, step=BLOCK, unroll=2)
         def _(r):
             r = pl.multiple_of(r, BLOCK)
             body(r, pl.ds(r, BLOCK))
@@ -791,13 +789,14 @@
     cols = mix_ref.shape[2]
     heads = cols // HEAD
 
-    @pl.when(t == 0)
-    def _():
-        gtok_ref[...] = gfirst_ref[...]
+    if gfirst_ref is not None:
+        @pl.when(t == 0)
+        def _():
+            gtok_ref[...] = gfirst_ref[...]
 
     bias_ref[...] = jnp.zeros_like(bias_ref)
 
-    @pl.loop(0, rows, step=BLOCK)
+    @pl.loop(0, rows, step=BLOCK, unroll=2)
     def _(r):
         r = pl.multiple_of(r, BLOCK)
         here = pl.ds(r, BLOCK)
@@ -857,7 +856,7 @@
         dqkv[here, 2 * cols :] = low
         bias_ref[0, 1:2, :] += jnp.sum(low.astype(F32), axis=0, keepdims=True)
 
-    @pl.loop(0, rows, step=BLOCK)
+    @pl.loop(0, rows, step=BLOCK, unroll=2)
     def _(r):
         r = pl.multiple_of(r, BLOCK)
         here = pl.ds(r, BLOCK)
@@ -922,6 +921,7 @@
     small = collect(3, small_acc.at[0], small_acc.at[1], small_rc, small_rb, small_ra, small_rz, "x")
     rest = CollectFlat(place, rest_acc, rest_rc, rest_rz, rest_rx, rest_ry, send.at[4], recv.at[4])
     tail = Tail(place, gs.at[3], tail_rx, tail_rz, tail_sz, tail_sx, send.at[5], recv.at[5])
+    begun = pltpu.make_async_copy(gfirst_ref, gtok_ref, home.at[4, 0])
     rows_y = (place.y, 1 - place.y)
     cut = down_acc.shape[3]
     head, foot = slice(0, cut), slice(cut, cut + rest_acc.shape[3])
@@ -945,6 +945,7 @@
     @pl.when(t == 0)
     def _():
         place.greet()
+        begun.start()
         begin(up, gup_ref, up_acc, 0)
         begin(down, gdn_ref, down_acc, 1, head)
         begin(rest, gdn_ref, rest_acc, 3, foot)
@@ -955,6 +956,7 @@
 
     @pl.when(t == 2)
     def _():
+        down.send_a()
         up.sum_b()
 
     @pl.when(t == 3)
@@ -982,14 +984,14 @@
         at(0, 1, up_first)
         at(0, 2, up.send_b)
         at(0, 3, down_first)
-        at(1, 3, down.sum_b)
         at(2, 0, up.send_a, attn.send_b)
         at(2, 1, rest.sum_z)
         at(2, 2, rest.send_x, down.sum_a)
-        at(2, 3, down.send_z, rest.sum_x)
+        at(2, 3, down.send_z)
+        at(0, 3, begun.wait)
         at(3, 0, up.send_z)
-        at(3, 1, lambda: down.sum_z(down_out.at[head]))
-        at(3, 2, lambda: rest.sum_y(down_out.at[foot]))
+        at(3, 1, rest.sum_x, lambda: down.sum_z(down_out.at[head]))
+        at(3, 2, rest.send_y)
 
     g = place.group(last - t)
 
@@ -1003,12 +1005,8 @@
 
         @pl.when(t == 1)
         def _():
-            down.send_a()
+            down.sum_b()
             attn.wait_c(1)
-
-        @pl.when(t == 2)
-        def _():
-            rest.send_y()
 
         @pl.when(t == last)
         def _():
@@ -1041,7 +1039,7 @@
 
     attend_back_steps(
         hook, before_grads, put,
-        x_ref, w_ref, gattn_ref, gfirst_ref, q_ref, k_ref, v_ref, mix_ref, lse_ref, gtok_ref, bias_ref,
+        x_ref, w_ref, gattn_ref, None, q_ref, k_ref, v_ref, mix_ref, lse_ref, gtok_ref, bias_ref,
         qh, gh, dq, kh, dqkv,
     )
 
@@ -1061,6 +1059,7 @@
         small.send_b()
         small.sum_b()
         small.send_a()
+        rest.sum_y(down_out.at[foot])
         up.finish()
         down.finish()
         rest.finish()
@@ -1270,7 +1269,7 @@
         grid=(groups,),
         in_specs=[
             resident(table.shape), resident((rows, width)), back(w_attn.shape),
-            resident((rows, width)), resident((rows, width)),
+            resident((rows, width)), pl.BlockSpec(memory_space=pl.ANY),
             back(q.shape), back(k.shape), back(v.shape), back(mixed.shape), back(lse.shape),
             resident(small.shape),
             pl.BlockSpec(memory_space=pl.ANY), pl.BlockSpec(memory_space=pl.ANY),
@@ -1292,7 +1291,7 @@
             pltpu.VMEM((DEPTH - 1, 2, 2, *half), BF16), pltpu.VMEM((2, *half), BF16), pltpu.VMEM(half, BF16),
             pltpu.VMEM((2, *pair, *dots), F32), pltpu.VMEM((*pair, *dots), F32), *buffers(dots, F32, "x"),
             pltpu.SemaphoreType.DMA((6, 8)), pltpu.SemaphoreType.DMA((6, 8)),
-            pltpu.SemaphoreType.DMA((4, 2)),
+            pltpu.SemaphoreType.DMA((5, 2)),
         ],
         compiler_params=pltpu.CompilerParams(
             dimension_semantics=("arbitrary",), vmem_limit_bytes=VMEM_LIMIT, collective_id=1,
@@ -1313,7 +1312,6 @@
     seq_count = lengths.shape[0]
     assert rows * groups == seq_count * rows and seq_count == groups
     rank = lax.axis_index("tensor")
-    length = lax.dynamic_slice_in_dim(lengths, rank, 1)
     both = ("dp", "tensor")
 
     cols = width // groups
@@ -1343,9 +1341,11 @@
         full = jnp.pad(full, ((0, 16 - full.shape[0]), (0, 0)))
         qb, vb = full[0].reshape(groups, 1, cols), full[1].reshape(groups, 1, cols)
         bias = jnp.pad(jnp.concatenate([qb, jnp.zeros_like(qb), vb], axis=2), ((0, 0), (0, 7), (0, 0)))
-        residual, q, k, v, mixed, lse = run_attend(length, tokens, w_attn, bias, full[2:3])
+        residual, q, k, v, mixed, lse = run_attend(
+            lax.dynamic_slice_in_dim(lengths, rank, 1), tokens, w_attn, bias, full[2:3]
+        )
     output, grad_first, grad_attn, small, grad_in, grad_back = run_ffn(
-        length, residual, cotangent, full, w_in, w_back
+        lengths, residual, cotangent, full, w_in, w_back
     )
     if near:
         split = (2, 2, DEPTH, 2, width // (2 * DEPTH), units)

time: 280 us -> 256 us (0.914)
  Pallas kernels: 263 us -> 240 us
    pallas_call x1, Pallas kernels: 115 us -> 104 us  [run_attend_back_collect(): pl.pallas_call(attend_back_collect_kernel, grid=(groups,), in_specs=[resi...]
    pallas_call x1, Pallas kernels: 87.1 us -> 79.2 us  [run_attend_spread(): pl.pallas_call(attend_spread_kernel, grid=(groups,), in_specs=[pl.BlockSp...]
    pallas_call x1, Pallas kernels: 60.4 us -> 57.1 us  [run_ffn(): pl.pallas_call(ffn_kernel, grid=(2, groups), in_specs=[pl.BlockSpec(memor...]
where the time goes in v5:
time: 256 us
  Pallas kernels  240 us (94%)
  local copies, waits for them, and re-layouts  13 us (5%)
    pallas_call x1, Pallas kernels, run_attend_back_collect(): pl.pallas_call(attend_back_collect_kernel, grid=(groups,), in_specs=[resi...  104 us
    pallas_call x1, Pallas kernels, run_attend_spread(): pl.pallas_call(attend_spread_kernel, grid=(groups,), in_specs=[pl.BlockSp...  79.2 us
    pallas_call x1, Pallas kernels, run_ffn(): pl.pallas_call(ffn_kernel, grid=(2, groups), in_specs=[pl.BlockSpec(memor...  57.1 us
    unnamed x11, local copies, waits for them, and re-layouts  6.89 us

profile of v5, /device:TPU:0, one launch (start us, length us, event | category | flops | bytes accessed | tf_op | source)
XLA Modules:
  0.0 255.6 jit_solution(2266548575113874678)
XLA Ops:
  0.7 0.8 stack.35
  1.5 0.8 scatter.4.own_vec
  2.2 0.0 copy-start.2
  2.3 0.9 copy.37
  3.2 1.6 pad_maximum_fusion.own_attn
  4.8 0.0 copy-done.2
  4.8 79.2 %attend.1 = (f32[1024,768]{1,0:T(8,128)}, bf16[4,1024,256]{2,1,0:T(8,128)(2,1)}, bf16[4,1024,256]{2,1,0:T(8,128)(2,1)}, bf16[4,1024,256]{2,1,0:T(8,128)(2,1)}, b...) custom-call(s32[4]{0:T(128)} %len_ref.3, ...), custom_call_target="tpu_custom_call" | custom-call | tf_op jit(solution)/shard_map/attend/pallas_call | solution.py:1147
  83.9 57.1 %ffn.1 = (f32[1024,768]{1,0:T(8,128)}, f32[1024,768]{1,0:T(8,128)}, bf16[1024,768]{1,0:T(8,128)(2,1)}, f32[16,768]{1,0:T(8,128)}, bf16[4,768,768]{2,1,0:T(8,128)(2,1)}, /*index=5*/bf16[4,768,768]{2,1,0:T(8,128)(2,1)}) custom-call(s32[4]{0:T(128)} %len_ref.3, f32[1024,768]{1,0:T(8,128)} %get-tuple-element.50.res_ref, bf16[1024,768]{1,0:T(8,128)(2,1)} %cot_ref.1, ...), custom_call_target="tpu_custom_call" | custom-call | tf_op jit(solution)/shard_map/ffn/pallas_call | solution.py:1182
  141.0 104.1 %attend_back.1 = (f32[1024,768]{1,0:T(8,128)}, f32[96,768]{1,0:T(8,128)}, f32[96,768]{1,0:T(8,128)}, f32[96,768]{1,0:T(8,128)}, f32[16,128]{1,0:T(8,128)}) custom-call(s32[8,768]{1,0:T(8,128)} %constant.34.clone.tab_ref, bf16[1024,768]{1,0:T(8,128)(2,1)} %x_ref.3, bf16[4,768,768]{2,1,0:T(8,128)(2,1)} %get-tuple-element.55.w_ref, ...), custom_call_target="tpu_custom_call" | custom-call | tf_op jit(solution)/shard_map/attend_back/pallas_call | solution.py:1267
  245.1 1.2 slice_bitcast_fusion.4
  246.3 1.5 slice_bitcast_fusion.1
  247.8 1.8 slice_bitcast_fusion
  249.6 0.7 copy.38
  250.4 0.0 copy-start.1
  250.4 0.0 copy-start
  250.4 3.8 %copy.43 = f32[1024,768]{1,0:T(8,128)} copy(f32[1024,768]{1,0:T(8,128)} %get-tuple-element.118) | data formatting | bytes 6291456
  254.2 0.0 copy-done.1
  254.2 0.7 copy.44
  254.9 0.0 copy-done
  254.9 0.7 copy.45
  (1 shorter events, 0.0 us)
Async XLA Ops:
  2.2 2.5 copy-start.2
  250.4 3.8 %copy-start.1 = (f32[96,768]{1,0:T(8,128)S(1)}, f32[96,768]{1,0:T(8,128)}, u32[]{:S(2)}) copy-start(f32[96,768]{1,0:T(8,128)} %get-tuple-element.123) | copy-start | bytes 884740
  250.4 4.5 %copy-start = (f32[96,768]{1,0:T(8,128)S(1)}, f32[96,768]{1,0:T(8,128)}, u32[]{:S(2)}) copy-start(f32[96,768]{1,0:T(8,128)} %get-tuple-element.69) | copy-start | bytes 884740
